TPU v7x, 512 devices: a whole 4x8x8 slice. The times are simulated.
512 devices in a mesh: gx: 8 (over z), gy: 8 (over y), gz: 8 (over x, core).
Axes of the slice: x: 4, y: 8, z: 8, core: 2. Of those that a mesh axis runs over, the one named last changes fastest.
Arguments:
- right_side: float32 [512, 512, 512], P('gx', 'gy', 'gz'), may hold values from -6 to 6
- guess: float32 [512, 512, 512], P('gx', 'gy', 'gz'), may hold values from -6 to 6
Outputs:
- solution: float32 [512, 512, 512], P('gx', 'gy', 'gz')
- residual: float32 [512, 512, 512], P('gx', 'gy', 'gz')
All inputs are finite; a program needn't handle non-finite values.
Results may differ from a plain program's by a relative error of at most 0.0003.
Values sent between devices are 32-bit elements.
No kernel may reach another device: no remote copies, remote signals or barrier semaphores. Data moves between devices by JAX's collectives and lax.ppermute only.
A program may use at most 256 MiB of HBM per device.

v0:
```python
import typing

import jax
import jax.numpy as jnp
from jax import lax
from jax.experimental import pallas as pl
from jax.experimental.pallas import tpu as pltpu
from jax.sharding import PartitionSpec as P


F32 = jnp.float32
BF16 = jnp.bfloat16
COARSE_SWEEPS = 4
COUNT = 8


class Level(typing.NamedTuple):
    level: int
    pairs: int
    rows: int
    first: int
    offset: int
    size: int

    @property
    def scale(self):
        return 4.0**self.level

    @property
    def inverse(self):
        return 0.25**self.level

    @property
    def own(self):
        return self.size // 2

    def shape(self):
        return (self.pairs + 2, self.rows, 128)


L0 = Level(0, 40, 80, 3, 8, 64)
L1 = Level(1, 30, 64, 7, 16, 32)
L2 = Level(2, 14, 32, 3, 8, 16)
L3_OWN = Level(3, 6, 16, 1, 4, 8)
L3 = Level(3, 12, 32, 4, 8, 8)
L4 = Level(4, 16, 32, 0, 0, 32)
L5 = Level(5, 8, 16, 0, 0, 16)
L6 = Level(6, 4, 8, 0, 0, 8)


class Edges(typing.NamedTuple):
    ilo: typing.Any
    ihi: typing.Any
    jlo: typing.Any
    jhi: typing.Any
    klo: typing.Any
    khi: typing.Any


def block_edges():
    ends = []
    for axis in ("gx", "gy", "gz"):
        place = lax.axis_index(axis)
        ends += [place == 0, place == COUNT - 1]
    return Edges(*ends)


def whole_edges():
    yes = lax.axis_index("gx") >= 0
    return Edges(*([yes] * 6))


def lanes_of(shape):
    return lax.broadcasted_iota(jnp.int32, shape, len(shape) - 1)


def rows_of(shape):
    return lax.broadcasted_iota(jnp.int32, shape, len(shape) - 2)


def signed(lane):
    return jnp.where(lane < 96, lane, lane - 128)


def cells_of(shape):
    row = rows_of(shape)
    return (row & 7) * (shape[-2] // 8) + (row >> 3)


def even_mask(rows):
    shape = (rows, 128)
    return ((cells_of(shape) + lanes_of(shape)) & 1) == 0


def even_natural(shape):
    return ((rows_of(shape) + lanes_of(shape)) & 1) == 0


def gather_rows(ref, index, rows, start=0):
    stride = rows // 8
    if stride == 1:
        return ref[index, pl.ds(start, 8), :]
    return jnp.concatenate([ref[index, pl.ds(start + t, 8, stride=stride), :] for t in range(stride)], axis=0)


def scatter_rows(ref, index, value, start=0):
    stride = value.shape[0] // 8
    for t in range(stride):
        ref[index, pl.ds(start + t, 8, stride=stride), :] = value[8 * t : 8 * t + 8]


def row_before(value):
    last = value[value.shape[0] - 8 :]
    first = jnp.where(rows_of((8, 128)) == 0, 0.0, pltpu.roll(last, 1, 0))
    return first if value.shape[0] == 8 else jnp.concatenate([first, value[: value.shape[0] - 8]], axis=0)


def row_after(value):
    last = jnp.where(rows_of((8, 128)) == 7, 0.0, pltpu.roll(value[:8], 7, 0))
    return last if value.shape[0] == 8 else jnp.concatenate([value[8:], last], axis=0)


def fold_rows(value):
    tiles = value.shape[0] // 16
    if tiles == 0:
        raise ValueError("rows")
    return jnp.concatenate([value[16 * t : 16 * t + 8] + value[16 * t + 8 : 16 * t + 16] for t in range(tiles)], axis=0)


def double_rows(even, odd):
    parts = []
    for t in range(even.shape[0] // 8):
        parts += [even[8 * t : 8 * t + 8], odd[8 * t : 8 * t + 8]]
    return jnp.concatenate(parts, axis=0)


def turn(value, shift, axis):
    size = value.shape[axis]
    if isinstance(shift, int):
        shift %= size
        if shift == 0:
            return value
    return pltpu.roll(value, shift, axis)


def bounds(low, high, size):
    return jnp.where(low, 0, -4096), jnp.where(high, size, 4096)


def set_coefficients(lv, edges, c_ref, d_ref):
    shape = (lv.rows, 128)
    row = cells_of(shape) - lv.offset
    lane = signed(lanes_of(shape))
    row_low, row_high = bounds(edges.jlo, edges.jhi, lv.size)
    lane_low, lane_high = bounds(edges.klo, edges.khi, lv.size)
    inside = (row >= row_low) & (row < row_high) & (lane >= lane_low) & (lane < lane_high)
    diagonal = 6.0 + jnp.where(row == row_low, 1.0, 0.0) + jnp.where(row == row_high - 1, 1.0, 0.0)
    diagonal = diagonal + jnp.where(lane == lane_low, 1.0, 0.0) + jnp.where(lane == lane_high - 1, 1.0, 0.0)
    even = jnp.where(even_mask(lv.rows), 1.0, 0.0)
    for index, extra in enumerate((0.0, even, 1.0 - even)):
        d_ref[index] = diagonal + extra
        c_ref[index] = jnp.where(inside, 1.0 / (diagonal + extra), 0.0)
    c_ref[3] = jnp.zeros(shape, F32)


def kind(lv, edges, p, red):
    last = lv.first + lv.own - 1
    low, high = (1, 2) if red else (2, 1)
    if isinstance(p, int):
        if p in (lv.first, last):
            return jnp.where(edges.ilo, low, 0) if p == lv.first else jnp.where(edges.ihi, high, 0)
        return 0 if lv.first < p < last else jnp.where(edges.ilo if p < lv.first else edges.ihi, 3, 0)
    inner = jnp.where((p == lv.first) & edges.ilo, low, jnp.where((p == last) & edges.ihi, high, 0))
    return jnp.where(((p < lv.first) & edges.ilo) | ((p > last) & edges.ihi), 3, inner)


def loop(low, high, body, width=0):
    count = high - low
    width = count if width == 0 else min(width, count)

    def step(n, carry):
        for k in range(width):
            body(low + n * width + k)
        return carry

    if count // width > 1:
        lax.fori_loop(0, count // width, step, 0)
        done = count // width * width
    else:
        done = 0
    for p in range(low + done, high):
        body(p)


def group(rows):
    return max(1, 180 // (rows // 8))


def neighbour_weights():
    shape = (256, 128)
    apart = ((rows_of(shape) & 127) - lanes_of(shape)) & 127
    return jnp.where((apart == 1) | (apart == 127), 1.0, 0.0).astype(BF16)


def lane_sum(value, weights):
    rows = value.shape[0]
    part = rows if weights is None else 16
    total = turn(value[:part], 1, 1) + turn(value[:part], 127, 1)
    return total if part == rows else jnp.concatenate([total, split_dot(value[part:], weights[...])], axis=0)


def around(ref, p, even, red, weights=None):
    value = ref[p + 1]
    before, after = ref[p], ref[p + 2]
    total = value + (jnp.where(even, before, after) if red else jnp.where(even, after, before))
    total = total + (row_before(value) + row_after(value))
    return total + lane_sum(value, weights)


def relax_at(lv, edges, c_ref, other, source, dest, p, red, even, weights=None):
    total = around(other, p, even, red, weights) + (source[p + 1] if lv.level == 0 else lv.scale * source[p + 1])
    dest[p + 1] = total * c_ref[kind(lv, edges, p, red)]


def relax(lv, edges, c_ref, other, source, dest, low, high, red):
    even = even_mask(lv.rows)
    loop(low, high, lambda p: relax_at(lv, edges, c_ref, other, source, dest, p, red, even), group(lv.rows))


def relax_zero(lv, edges, c_ref, source, dest, low, high):
    def body(p):
        dest[p + 1] = lv.scale * source[p + 1] * c_ref[kind(lv, edges, p, True)]

    loop(low, high, body, group(lv.rows))


def gap(lv, d, value, total):
    return d * value - total if lv.level == 0 else lv.inverse * (d * value - total)


def black_rest_at(lv, edges, c_ref, d_ref, red, source, dest, rest, p, even, weights=None):
    total = around(red, p, even, False, weights)
    g = source[p + 1]
    at = kind(lv, edges, p, False)
    value = (total + (g if lv.level == 0 else lv.scale * g)) * c_ref[at]
    dest[p + 1] = value
    rest[p + 1] = g - gap(lv, d_ref[jnp.minimum(at, 2)], value, total)


def relax_black_rest(lv, edges, c_ref, d_ref, red, source, dest, rest, low, high):
    even = even_mask(lv.rows)
    loop(low, high, lambda p: black_rest_at(lv, edges, c_ref, d_ref, red, source, dest, rest, p, even), group(lv.rows))


def red_rest(lv, edges, d_ref, source, red, black, p, even, weights=None):
    d = d_ref[jnp.minimum(kind(lv, edges, p, True), 2)]
    return source[p + 1] - gap(lv, d, red[p + 1], around(black, p, even, True, weights))


def clear_guards(*refs):
    for ref in refs:
        ref[0] = jnp.zeros(ref.shape[1:], F32)
        ref[ref.shape[0] - 1] = jnp.zeros(ref.shape[1:], F32)


def split_dot(value, weights):
    high = value.astype(BF16)
    low = (value - high.astype(F32)).astype(BF16)
    return jnp.dot(jnp.concatenate([high, low], axis=1), weights, preferred_element_type=F32)


def halving_weights(own_lanes):
    shape = (256, 128)
    fine = signed(rows_of(shape) & 127)
    coarse = signed(lanes_of(shape))
    hit = (fine >> 1) == coarse
    if own_lanes:
        hit = hit & (fine >= 0) & (fine < own_lanes)
    return jnp.where(hit, 0.125, 0.0).astype(BF16)


def doubling_weights(size, low, high):
    shape = (256, 256)
    coarse = signed(rows_of(shape) & 127)
    lane = lanes_of(shape)
    fine = signed(lane & 127)
    parent = fine >> 1
    beside = parent + jnp.where((fine & 1) == 1, 1, -1)
    beyond = ((beside == -1) & low) | ((beside == size) & high)
    centre = jnp.where(coarse == parent, 0.25, 0.0)
    neighbour = jnp.where(coarse == beside, 0.25, 0.0)
    mixed = jnp.where(beyond, 0.0, centre + neighbour)
    return jnp.where(lane < 128, mixed, centre).astype(BF16)


def rest_fold_at(lv, edges, d_ref, g_red, red, black, rest, low, z_ref, p, even, weights=None):
    z_ref[p - low] = fold_rows(rest[p + 1] + red_rest(lv, edges, d_ref, g_red, red, black, p, even, weights))


def restrict(lv, edges, d_ref, g_red, red, black, rest, low, count, z_ref, out_ref, weights):
    even = even_mask(lv.rows)
    loop(
        low, low + count,
        lambda p: rest_fold_at(lv, edges, d_ref, g_red, red, black, rest, low, z_ref, p, even), group(lv.rows),
    )
    halve(lv, count, z_ref, out_ref, weights)


def halve(lv, count, z_ref, out_ref, weights):
    half = lv.rows // 2
    chunk = max(c for c in range(1, count + 1) if count % c == 0 and (c * half <= 320 or c == 1))

    def product(n):
        value = z_ref[pl.ds(n * chunk, chunk)].reshape(chunk * half, 128)
        out_ref[pl.ds(n * chunk, chunk)] = split_dot(value, weights[...]).reshape(chunk, half, 128)

    loop(0, count // chunk, product)


def colour_planes(planes, pairs, red, black):
    even = even_mask(planes.shape[1])

    def body(p):
        low, high = planes[2 * p], planes[2 * p + 1]
        red[p + 1] = jnp.where(even, low, high)
        black[p + 1] = jnp.where(even, high, low)

    loop(0, pairs, body, 8)


def whole_planes(lv, red, black, pair_low, pairs, e_ref):
    even = even_mask(lv.rows)

    def body(t):
        r, b = red[pair_low + t + 1], black[pair_low + t + 1]
        e_ref[2 * t] = jnp.where(even, r, b)
        e_ref[2 * t + 1] = jnp.where(even, b, r)

    loop(0, pairs, body, 8)


def window_planes(lv, red, black, pair_low, pairs, row_low, natural, e_ref):
    even = even_mask(lv.rows)
    rows = e_ref.shape[1]

    def body(t):
        r, b = red[pair_low + t + 1], black[pair_low + t + 1]
        scatter_rows(natural, 2 * t, jnp.where(even, r, b))
        scatter_rows(natural, 2 * t + 1, jnp.where(even, b, r))

    def again(t):
        e_ref[t] = gather_rows(natural, t, rows, row_low)

    loop(0, pairs, body, 4)
    loop(0, 2 * pairs, again, 8)


def prolong(e_ref, count, plane_zero, size, edges, weights, mixed, plain):
    rows = e_ref.shape[1]
    chunk = max(c for c in range(1, count + 1) if count % c == 0 and (c * rows <= 320 or c == 1))

    def body(n):
        at = pl.ds(n * chunk, chunk)
        both = split_dot(e_ref[at].reshape(chunk * rows, 128), weights[...])
        mixed[at] = both[:, :128].reshape(chunk, rows, 128)
        plain[at] = both[:, 128:].reshape(chunk, rows, 128)

    loop(0, count // chunk, body)
    if plane_zero > 0:
        pl.when(edges.ilo)(lambda: plain.__setitem__(plane_zero - 1, -plain[plane_zero]))
    last = plane_zero + size - 1
    if last + 1 < count:
        pl.when(edges.ihi)(lambda: plain.__setitem__(last + 1, -plain[last]))


def correct(lv, edges, c_ref, kept, mixed, plain, row_zero, plane_zero, dest, low, high):
    body = correct_at(lv, edges, c_ref, kept, mixed, plain, row_zero, plane_zero, dest)
    loop(low, high, body, group(lv.rows))


def correct_at(lv, edges, c_ref, kept, mixed, plain, row_zero, plane_zero, dest):
    even = even_mask(lv.rows)
    half = lv.rows // 2
    row = cells_of((half, 128)) - row_zero
    at_low = (row == 0) & edges.jlo
    at_high = (row == lv.size // 2 - 1) & edges.jhi

    def body(p):
        t = p - lv.first + plane_zero
        value, near = plain[t], mixed[t]
        before = near + jnp.where(at_low, -value, row_before(value))
        after = near + jnp.where(at_high, -value, row_after(value))
        up, down = plain[t + 1], plain[t - 1]
        step = double_rows(before, after) + jnp.where(even, double_rows(up, up), double_rows(down, down))
        c = c_ref[kind(lv, edges, p, False)]
        dest[p + 1] = jnp.where(c > 0.0, kept[p + 1] + step, 0.0)

    return body


def compact_kernel(guess, source, x_ref, y_ref):
    even = ((rows_of((64, 64)) + lanes_of((64, 64))) & 1) == 0

    def body(u):
        blacks = []
        for s in range(2):
            p = 2 * u + s
            low, high = guess[2 * p], guess[2 * p + 1]
            f_low, f_high = source[2 * p], source[2 * p + 1]
            x_ref[p] = jnp.concatenate([jnp.where(even, high, low), jnp.where(even, f_low, f_high)], axis=1)
            blacks.append(jnp.where(even, f_high, f_low))
        y_ref[u] = jnp.concatenate(blacks, axis=1)

    loop(0, 16, body, 2)


def pack_kernel(ib, ia, x, y, jb, ja, xf, yf, ku, kd):
    zero = jnp.zeros((80, 128), F32)
    for p in range(3):
        xf[p, 8:72] = ib[p]
        xf[35 + p, 8:72] = ia[p]
    loop(0, 32, lambda p: xf.__setitem__((p + 3, slice(8, 72)), x[p]), 4)
    yf[0, 8:72] = ib[3]
    yf[17, 8:72] = ia[3]
    loop(0, 16, lambda p: yf.__setitem__((p + 1, slice(8, 72)), y[p]), 4)

    tile = jnp.zeros((8, 128), F32)
    for p in range(38):
        xf[p, 0:8] = tile
        xf[p, 3:8] = jb[5 * p : 5 * p + 5]
        xf[p, 72:80] = tile
        xf[p, 72:77] = ja[5 * p : 5 * p + 5]
    for p in range(18):
        yf[p, 0:8] = tile
        yf[p, 5:8] = jb[190 + 3 * p : 193 + 3 * p]
        yf[p, 72:80] = tile
        yf[p, 72:75] = ja[190 + 3 * p : 193 + 3 * p]
    for p in (38, 39):
        xf[p] = zero
    for p in range(18, 24):
        yf[p] = zero
    lane = lanes_of((80, 128))
    for u in range(5):
        down, up, up_y = zero, zero, zero
        for s in range(8):
            value = turn(xf[8 * u + s], 8 * s, 1)
            place = (lane - 8 * s) & 127
            down = jnp.where((place < 5) | ((place >= 64) & (place < 68)), value, down)
            up = jnp.where(((place >= 59) & (place < 64)) | (place >= 124), value, up)
            if 8 * u + s < 18:
                value = turn(yf[8 * u + s], 8 * s + 5, 1)
                down = jnp.where(place_y(lane, s, 0), value, down)
                up_y = jnp.where(place_y(lane, s, 61), value, up_y)
        kd[u] = down
        ku[u] = up + turn(up_y, -2, 1) if u < 3 else up


def place_y(lane, s, start):
    place = (lane - 8 * s - 5) & 63
    return (place >= start) & (place < start + 3)


def rows_kernel(ib, ia, guess_low, guess_high, source_low, source_high, up, down):
    even = even_natural((8, 64))
    for out, guess, source, low, x_at, y_at in (
        (down, guess_low, source_low, 0, 0, 0),
        (up, guess_high, source_high, 56, 3, 5),
    ):
        blacks = []
        for p in range(38):
            if 3 <= p < 35:
                n = 2 * p - 6
                first, second, f_first, f_second = guess[n], guess[n + 1], source[n], source[n + 1]
                value = jnp.concatenate(
                    [jnp.where(even, second, first), jnp.where(even, f_first, f_second)], axis=1
                )
                blacks.append(jnp.where(even, f_second, f_first))
            else:
                value = ib[p, low : low + 8] if p < 3 else ia[p - 35, low : low + 8]
            out[5 * p : 5 * p + 5] = value[x_at : x_at + 5]
        for p in range(18):
            if p == 0 or p == 17:
                value = (ib if p == 0 else ia)[3, low : low + 8]
            else:
                value = jnp.concatenate(blacks[2 * p - 2 : 2 * p], axis=1)
            out[190 + 3 * p : 193 + 3 * p] = value[y_at : y_at + 3]
        out[244:248] = jnp.zeros((4, 128), F32)


def spread_kernel(xf, yf, black, g_red, g_black, c_ref, d_ref, weights, lanes):
    set_coefficients(L0, block_edges(), c_ref, d_ref)
    weights[...] = halving_weights(64)
    lanes[...] = neighbour_weights()
    zero = jnp.zeros((80, 128), F32)
    own = lanes_of((80, 128)) < 64

    def first(p):
        value = gather_rows(xf, p, 80)
        black[p + 1] = jnp.where(own, value, 0.0)
        g_red[p + 1] = jnp.where(own, turn(value, 64, 1), 0.0)

    loop(0, 40, first, 4)

    def second(p):
        value = gather_rows(yf, p, 80)
        g_black[2 * p + 2] = jnp.where(own, value, 0.0)
        g_black[2 * p + 3] = jnp.where(own, turn(value, 64, 1), 0.0)

    loop(0, 18, second, 4)
    for q in (0, 1, 38, 39, 40, 41):
        g_black[q] = zero
    clear_guards(black, g_red)


def fine_kernel(
    black0, g_red0, g_black0, kb, ka, c_ref, d_ref, weights, lanes, v_black, g_red, g_black, low_quads, high_quads,
    black, red, rest, z_ref, planes, natural,
):
    edges = block_edges()
    zero = jnp.zeros((80, 128), F32)
    lane = lanes_of((80, 128))

    even = even_mask(80)

    def sides(u):
        below = jnp.where(edges.klo, 0.0, gather_rows(kb, u, 80))
        return below, jnp.where(edges.khi, 0.0, gather_rows(ka, u, 80))

    def merge(p):
        below, above = sides(p // 8)
        turned = 8 * (p % 8)
        place = (lane - turned) & 127
        edge = jnp.where(place < 5, above, jnp.where((place >= 59) & (place < 64), below, 0.0))
        black[p + 1] = black0[p + 1] + turn(edge, 64 - turned, 1)
        edge = jnp.where((place >= 64) & (place < 68), above, jnp.where(place >= 124, below, 0.0))
        g_red[p + 1] = g_red0[p + 1] + turn(edge, -turned, 1)

    def merge_black(n):
        below, above = sides(n // 8)
        below = turn(below, 2, 1)
        turned = 8 * (n % 8)
        place = (lane - turned) & 127
        edge = jnp.where((place >= 5) & (place < 8), above, jnp.where((place >= 66) & (place < 69), below, 0.0))
        g_black[2 * n + 2] = g_black0[2 * n + 2] + turn(edge, 59 - turned, 1)
        edge = jnp.where((place >= 69) & (place < 72), above, jnp.where((place >= 2) & (place < 5), below, 0.0))
        g_black[2 * n + 3] = g_black0[2 * n + 3] + turn(edge, -5 - turned, 1)

    for q in (0, 1, 38, 39, 40, 41):
        g_black[q] = zero
    for ref in (black, g_red):
        for q in (0, 39, 40, 41):
            ref[q] = zero
    for ref in (red, v_black):
        for q in (0, 1, 38, 39, 40, 41):
            ref[q] = zero
    for n in range(44):
        if n < 38:
            merge(n)
        if n % 2 == 0 and n < 36:
            merge_black(n // 2)
        if 1 <= n - 2 < 37:
            relax_at(L0, edges, c_ref, black, g_red, red, n - 2, True, even, lanes)
        if 1 <= n - 4 < 37:
            black_rest_at(L0, edges, c_ref, d_ref, red, g_black, v_black, rest, n - 4, even, lanes)
        if 3 <= n - 6 < 35:
            rest_fold_at(L0, edges, d_ref, g_red, red, v_black, rest, 3, z_ref, n - 6, even, lanes)
    halve(L0, 32, z_ref, planes, weights)

    def quad(q):
        total = planes[4 * q]
        for m in range(1, 4):
            total = total + turn(planes[4 * q + m], 32 * m, 1)
        scatter_rows(natural, q, total)
        return natural[q, 4:36]

    for q in range(4):
        low_quads[q] = quad(q)
        high_quads[q] = quad(q + 4)


def quad_rows(ib, ia, low_quads, high_quads, jb, ja, q):
    own = (ib, low_quads, high_quads, ia)[q // 4][q % 4]
    return jnp.concatenate([jb[q], own, ja[q]], axis=0)


def pack_quads_kernel(ib, ia, low_quads, high_quads, jb, ja, ku, kd):
    low_half = (lanes_of((64, 128)) & 31) < 16
    for u in range(8):
        first, second = (quad_rows(ib, ia, low_quads, high_quads, jb, ja, 2 * u + k) for k in range(2))
        kd[u] = turn(jnp.where(low_half, first, turn(second, 16, 1)), 32, 1)
        ku[u] = turn(jnp.where(low_half, turn(first, -16, 1), second), -32, 1)


def join_kernel(ib, ia, low_quads, high_quads, jb, ja, qf):
    for q in range(16):
        qf[q] = quad_rows(ib, ia, low_quads, high_quads, jb, ja, q)


WINDOWS = (L1, L2, L3_OWN, L3)
WHOLES = (L4, L5, L6)
DOUBLINGS = ((32, False), (16, False), (8, False), (4, False), (16, True), (8, True))


def geometry_kernel(after, *refs):
    edges, whole = block_edges(), whole_edges()
    for index, lv in enumerate(WINDOWS + WHOLES):
        set_coefficients(lv, edges if lv in WINDOWS else whole, refs[2 * index], refs[2 * index + 1])
    refs = refs[2 * len(WINDOWS + WHOLES) :]
    refs[0][...] = halving_weights(0)
    for n, (size, is_whole) in enumerate(DOUBLINGS):
        at = whole if is_whole else edges
        refs[1][n] = doubling_weights(size, at.klo, at.khi)


def middle_kernel(
    qf, kb, ka, c1, d1, c2, d2, c3, d3, weights, lanes, v1, gr1, gb1, v2, gr2, gb2, message,
    red1, y1, z1, p1, red2, y2, z2, p2, gr3, gb3, red3, black3, y3, z3, p3, natural,
):
    edges = block_edges()
    lane = lanes_of((64, 128))
    even = even_mask(64)

    def unpack(u):
        below = jnp.where(edges.klo, 0.0, gather_rows(kb, u, 64))
        above = jnp.where(edges.khi, 0.0, gather_rows(ka, u, 64))
        sides = ((turn(below, 16, 1), above), (below, turn(above, -16, 1)))
        for h in range(2):
            value = gather_rows(qf, 2 * u + h, 64)
            left, right = sides[h]
            for t in range(2):
                both = []
                for m in (2 * t, 2 * t + 1):
                    place = (lane - 32 * m) & 127
                    edge = jnp.where(place < 48, right, jnp.where(place >= 112, left, 0.0))
                    both.append(turn(jnp.where(place < 32, value, edge), -32 * m, 1))
                index = 4 * u + 2 * h + t
                gr1[index] = jnp.where(even, both[0], both[1])
                gb1[index] = jnp.where(even, both[1], both[0])

    clear_guards(red1, v1)
    for n in range(36):
        if n % 4 == 0 and n < 32:
            unpack(n // 4)
        p = n - 1
        if 0 <= p < 30:
            red1[p + 1] = L1.scale * gr1[p + 1] * c1[kind(L1, edges, p, True)]
        if 0 <= n - 3 < 30:
            black_rest_at(L1, edges, c1, d1, red1, gb1, v1, y1, n - 3, even, lanes)
        if 1 <= n - 5 < 29:
            rest_fold_at(L1, edges, d1, gr1, red1, v1, y1, 1, z1, n - 5, even, lanes)
    halve(L1, 28, z1, p1, weights)
    colour_planes(p1, 14, gr2, gb2)
    clear_guards(red2, v2, gr2, gb2)
    relax_zero(L2, edges, c2, gr2, red2, 0, 14)
    relax_black_rest(L2, edges, c2, d2, red2, gb2, v2, y2, 0, 14)
    restrict(L2, edges, d2, gr2, red2, v2, y2, 1, 12, z2, p2, weights)
    colour_planes(p2, 6, gr3, gb3)
    clear_guards(red3, black3)
    relax_zero(L3_OWN, edges, c3, gr3, red3, 0, 6)
    relax_black_rest(L3_OWN, edges, c3, d3, red3, gb3, black3, y3, 0, 6)
    restrict(L3_OWN, edges, d3, gr3, red3, black3, y3, 1, 4, z3, p3, weights)
    lane = lanes_of((8, 128))
    row = rows_of((8, 128))
    third = jnp.zeros((8, 128), F32)
    for i in range(8):
        scatter_rows(natural, i, p2[i + 2])
        third = third + turn(jnp.where(lane < 8, natural[i, 4:12], 0.0), 8 * i, 1)
    folded = third + turn(turn(third, 4, 0), 64, 1)
    blocks = jnp.zeros((8, 128), F32)
    for i in range(4):
        blocks = blocks + turn(jnp.where(lane < 4, p3[i], 0.0), 16 * i, 1)
    fourth = jnp.zeros((8, 128), F32)
    for r in range(4):
        fourth = jnp.where((lane & 15) >> 2 == r, turn(turn(blocks, 4 * r, 1), -2 - r, 0), fourth)

    def store(n):
        for r in range(4):
            message[n, r] = folded[r : r + 1]
        message[n, 4] = fourth[0:1]

    loop(0, 64, store, 8)


def plane_kernel(tiles, message, near, rows, grid, blocks):
    x, y, z = (lax.axis_index(axis) for axis in ("gx", "gy", "gz"))
    shape = (8, 128)
    lane, row = lanes_of(shape), rows_of(shape)

    for n in range(64):
        rows[n : n + 1] = tiles[n, 4]
    parts = [jnp.zeros(shape, F32)] * 4
    for n in range(8):
        value = rows[pl.ds(n, 8, stride=8), :]
        here = (lane & 31) >> 2 == n
        for r in range(4):
            index = (lane >> 5) * 16 + 4 * r + (lane & 3)
            parts[r] = jnp.where(here, jnp.take_along_axis(value, index, axis=1), parts[r])
    for r in range(4):
        grid[pl.ds(r, 8, stride=4), :] = parts[r]

    lane = signed(lane)
    for dy in range(3):
        sides = []
        for dz in range(3):
            yy, zz = y + (dy - 1), z + (dz - 1)
            inside = (yy >= 0) & (yy < COUNT) & (zz >= 0) & (zz < COUNT)
            index = jnp.clip(yy, 0, COUNT - 1) * COUNT + jnp.clip(zz, 0, COUNT - 1)
            for r in range(4):
                blocks[3 * dy + dz, r : r + 1] = tiles[index, r]
            value = blocks[3 * dy + dz]
            value = jnp.where(row < 4, value, turn(turn(value, 4, 0), 64, 1))
            sides.append(jnp.where(inside, value, 0.0))
        for i in range(8):
            total = jnp.zeros(shape, F32)
            for dz in range(3):
                hit = (lane >= 8 * (dz - 1)) & (lane < 8 * dz)
                total = jnp.where(hit, turn(sides[dz], 8 * (dz - 1) - 8 * i, 1), total)
            near[i, 8 * dy : 8 * dy + 8] = total

    wide = lanes_of((24, 128))
    ends = []
    for first in (2, 0):
        total = jnp.zeros((24, 128), F32)
        for n in range(6):
            hit = (wide >= 20 * n) & (wide < 20 * n + 20)
            total = jnp.where(hit, turn(near[first + n], 20 * n + 6, 1), total)
        ends.append(total)
    for n in range(COUNT):
        message[n, 0:32] = grid[...]
        message[n, 32:56] = jnp.where(x < n, ends[0], ends[1])


def coarse_kernel(
    tiles, near, v2, gr2, gb2, v1, gr1, gb1, v0, gr0, gb0, c0, d0, c1, c2, c3, c4, d4, c5, d5, c6, halving, doubling, lanes, out, rest,
    gr4, gb4, red4, v4, y4, z4, p4, gr5, gb5, red5, v5, y5, z5, p5, gr6, gb6, red6, v6, full,
    gr3, gb3, red3, v3, b3, b2, red2, b1, red1, b0, red0, y0, e_ref, mixed, plain, fine_mixed, fine_plain, natural, last, out_held, rest_held, sems,
):
    edges = block_edges()
    whole = whole_edges()
    x, y, z = (lax.axis_index(axis) for axis in ("gx", "gy", "gz"))

    lane = signed(lanes_of((24, 128)))
    even = even_natural((24, 128))
    empty = jnp.zeros((24, 128), F32)

    def put(index, low, high):
        natural[index, 0:24] = jnp.where(even, low, high)
        natural[index + 12, 0:24] = jnp.where(even, high, low)

    for n in range(4):
        put(4 + n, near[2 * n], near[2 * n + 1])
    put(0, empty, empty)
    put(11, empty, empty)
    for at, first in ((x - 1, 1), (x + 1, 8)):
        inside = (at >= 0) & (at < COUNT)
        value = jnp.where(inside, tiles[jnp.clip(at, 0, COUNT - 1), 32:56], 0.0)
        planes = [jnp.where((lane >= -6) & (lane < 14), turn(value, -20 * n - 6, 1), 0.0) for n in range(6)]
        for n in range(3):
            put(first + n, planes[2 * n], planes[2 * n + 1])
    for n in range(24):
        natural[n, 24:32] = jnp.zeros((8, 128), F32)
    for n in range(12):
        gr3[n + 1] = gather_rows(natural, n, 32)
        gb3[n + 1] = gather_rows(natural, n + 12, 32)
    clear_guards(red3, v3)
    relax_zero(L3, edges, c3, gr3, red3, 0, 12)
    relax(L3, edges, c3, red3, gb3, v3, 0, 12, False)

    lane = lanes_of((32, 128))
    even32 = even_mask(32)
    zero = jnp.zeros((8, 128), F32)

    def place(n):
        value = gather_rows(tiles, n, 32)
        for t in range(2):
            low = jnp.where(lane < 32, turn(value, -64 * t, 1), 0.0)
            high = jnp.where(lane < 32, turn(value, -64 * t - 32, 1), 0.0)
            index = 2 * n + t + 1
            gr4[index] = jnp.where(even32, low, high)
            gb4[index] = jnp.where(even32, high, low)

    loop(0, 8, place, 4)
    clear_guards(red4, v4, gr4, gb4)
    relax_zero(L4, whole, c4, gr4, red4, 0, 16)
    relax_black_rest(L4, whole, c4, d4, red4, gb4, v4, y4, 0, 16)
    restrict(L4, whole, d4, gr4, red4, v4, y4, 0, 16, z4, p4, halving)
    colour_planes(p4, 8, gr5, gb5)
    clear_guards(red5, v5, gr5, gb5)
    relax_zero(L5, whole, c5, gr5, red5, 0, 8)
    relax_black_rest(L5, whole, c5, d5, red5, gb5, v5, y5, 0, 8)
    restrict(L5, whole, d5, gr5, red5, v5, y5, 0, 8, z5, p5, halving)
    colour_planes(p5, 4, gr6, gb6)
    clear_guards(red6, v6)
    relax_zero(L6, whole, c6, gr6, red6, 0, 4)
    relax(L6, whole, c6, red6, gb6, v6, 0, 4, False)
    for _ in range(COARSE_SWEEPS - 1):
        relax(L6, whole, c6, v6, gr6, red6, 0, 4, True)
        relax(L6, whole, c6, red6, gb6, v6, 0, 4, False)

    def ascend(coarse, fine, c, w, coarse_red, coarse_black, kept, g_red, g_black, red):
        count = coarse.size
        e, rows = e_ref.at[0:count, 0:count], slice(0, count)
        n, p = mixed.at[0 : count + 2, rows], plain.at[0 : count + 2, rows]
        whole_planes(coarse, coarse_red, coarse_black, 0, coarse.pairs, e)
        prolong(e, count, 0, count, whole, w, mixed.at[1 : count + 1, rows], plain.at[1 : count + 1, rows])
        p[0] = -p[1]
        p[count + 1] = -p[count]
        correct(fine, whole, c, kept, n, p, 0, 1, kept, 0, fine.pairs)
        relax(fine, whole, c, kept, g_red, red, 0, fine.pairs, True)
        relax(fine, whole, c, red, g_black, kept, 0, fine.pairs, False)

    ascend(L6, L5, c5, doubling.at[5], red6, v6, v5, gr5, gb5, red5)
    ascend(L5, L4, c4, doubling.at[4], red5, v5, v4, gr4, gb4, red4)

    even = even_mask(32)
    for t in (0, 1, 2, 3, 36, 37, 38, 39):
        full[t] = jnp.zeros((48, 128), F32)

    def expand(t):
        r, b = red4[t + 1], v4[t + 1]
        for n, value in ((2 * t + 4, jnp.where(even, r, b)), (2 * t + 5, jnp.where(even, b, r))):
            full[n, 0:8] = zero
            scatter_rows(full, n, value, 8)
            full[n, 40:48] = zero

    loop(0, 16, expand, 4)

    def cut(t):
        rows = gather_rows(full, 4 * x + t, 16, 4 * y + 4)
        e_ref[t, 0:16] = pltpu.roll(rows, (128 - 4 * z) & 127, 1)

    loop(0, 12, cut)

    def lift(index, fine, c, count, rows, plane_zero, row_zero, size, kept, dest, low, high):
        e = e_ref.at[0:count, 0:rows]
        n, p = mixed.at[0:count, 0:rows], plain.at[0:count, 0:rows]
        prolong(e, count, plane_zero, size, edges, doubling.at[index], n, p)
        correct(fine, edges, c, kept, n, p, row_zero, plane_zero, dest, low, high)

    def smooth(lv, c, black, g_red, g_black, red, low, high, low2, high2):
        relax(lv, edges, c, black, g_red, red, low, high, True)
        relax(lv, edges, c, red, g_black, black, low2, high2, False)

    lift(3, L3, c3, 12, 16, 4, 4, 4, v3, b3, 1, 11)
    clear_guards(b3, red3)
    smooth(L3, c3, b3, gr3, gb3, red3, 2, 10, 2, 10)

    window_planes(L3, red3, b3, 2, 8, 4, natural.at[0:16, 0:32], e_ref.at[0:16, 0:16])
    lift(2, L2, c2, 16, 16, 4, 4, 8, v2, b2, 0, 14)
    clear_guards(b2, red2)
    smooth(L2, c2, b2, gr2, gb2, red2, 1, 13, 1, 13)

    whole_planes(L2, red2, b2, 1, 12, e_ref.at[0:24, 0:32])
    e = e_ref.at[0:24, 0:32]
    n, p = mixed.at[0:24, 0:32], plain.at[0:24, 0:32]
    prolong(e, 24, 4, 16, edges, doubling.at[1], n, p)
    correct1 = correct_at(L1, edges, c1, v1, n, p, 8, 4, b1)
    for index in (5, 26):
        b1[index] = jnp.zeros(b1.shape[1:], F32)
    even1 = even_mask(64)
    even0 = even_mask(80)
    mixed0, plain0 = fine_mixed, fine_plain
    correct0 = correct_at(L0, edges, c0, v0, mixed0, plain0, 4, 4, b0)
    b0[1] = jnp.zeros(b0.shape[1:], F32)
    b0[38] = jnp.zeros(b0.shape[1:], F32)
    copies = []

    def send(held, target, n):
        copy = pltpu.make_async_copy(held.at[pl.ds(8 * n, 8)], target.at[pl.ds(8 * n, 8)], sems.at[len(copies)])
        copy.start()
        copies.append(copy)

    def store(held, p, r, b):
        for n, value in ((0, jnp.where(even0, r, b)), (1, jnp.where(even0, b, r))):
            scatter_rows(last, 2 * (p & 7) + n, value)
            held[2 * p - 6 + n] = last[2 * (p & 7) + n, 8:72, 0:64]

    def coarse_step(n):
        if n < 25:
            correct1(n)
        if 5 <= n - 2 < 25:
            relax_at(L1, edges, c1, b1, gr1, red1, n - 2, True, even1, lanes)
        if 6 <= n - 4 < 24:
            relax_at(L1, edges, c1, red1, gb1, b1, n - 4, False, even1)

    def lift_planes(c):
        planes = []
        for t in range(4 * c, 4 * c + 4):
            r, b = red1[t + 6], b1[t + 6]
            scatter_rows(natural, 2 * t, jnp.where(even1, r, b))
            scatter_rows(natural, 2 * t + 1, jnp.where(even1, b, r))
            planes += [gather_rows(natural, 2 * t + k, 40, 12) for k in range(2)]
        both = split_dot(jnp.concatenate(planes, axis=0), doubling[0])
        for k in range(8):
            mixed0[8 * c + k] = both[40 * k : 40 * k + 40, :128]
            plain0[8 * c + k] = both[40 * k : 40 * k + 40, 128:]
        if c == 0:
            plain0[3] = jnp.where(edges.ilo, -plain0[4], plain0[3])
        if c == 4:
            plain0[36] = jnp.where(edges.ihi, -plain0[35], plain0[36])

    def fine_step(n):
        if n < 37:
            correct0(n)
        if 1 <= n - 2 < 37:
            relax_at(L0, edges, c0, b0, gr0, red0, n - 2, True, even0, lanes)
        p = n - 4
        if 2 <= p < 36:
            black_rest_at(L0, edges, c0, d0, red0, gb0, b0, y0, p, even0)
        if 3 <= p < 35:
            store(out_held, p, red0[p + 1], b0[p + 1])
            if p % 4 == 2:
                send(out_held, out, p // 4 - 1)
        p = n - 6
        if 3 <= p < 35:
            store(rest_held, p, red_rest(L0, edges, d0, gr0, red0, b0, p, even0), y0[p + 1])
            if p % 4 == 2:
                send(rest_held, rest, p // 4 - 1)

    done, ready = 0, 0
    for n in range(5, 29):
        coarse_step(n)
        for _ in range(2):
            if done < ready:
                done += 1
                fine_step(done)
        if n >= 12 and n % 4 == 0:
            lift_planes(n // 4 - 3)
            ready = 2 * n - 19
    for n in range(done + 1, 43):
        fine_step(n)
    for copy in copies:
        copy.wait()


def struct(*shape):
    return jax.ShapeDtypeStruct(shape, F32)


def call(kernel, outs, scratch, flops=2_000_000, out_space=pltpu.VMEM, semaphores=0):
    space = pl.BlockSpec(memory_space=pltpu.VMEM)
    extra = [pltpu.SemaphoreType.DMA((semaphores,))] if semaphores else []

    def run(*args):
        return pl.pallas_call(
            kernel,
            out_shape=outs,
            in_specs=[space] * len(args),
            out_specs=[pl.BlockSpec(memory_space=out_space)] * len(outs),
            scratch_shapes=[pltpu.VMEM(shape, F32) for shape in scratch] + extra,
            compiler_params=pltpu.CompilerParams(vmem_limit_bytes=40 * 2**20),
            cost_estimate=pl.CostEstimate(flops=flops, bytes_accessed=1_000_000, transcendentals=0),
        )(*args)

    return run


def pair(to_next, to_before, axis, ring=False):
    up = [(i, (i + 1) % COUNT) for i in range(COUNT if ring else COUNT - 1)]
    down = [(j, i) for i, j in up]
    after = lax.ppermute(to_before, axis, down)
    before = lax.ppermute(to_next, axis, up)
    return before, after


def face(guess, source, start, first):
    even = ((lax.broadcasted_iota(jnp.int32, (64, 64), 0) + lax.broadcasted_iota(jnp.int32, (64, 64), 1)) & 1) == 0
    low, high = guess[start : start + 6 : 2], guess[start + 1 : start + 6 : 2]
    f_low, f_high = source[start : start + 6 : 2], source[start + 1 : start + 6 : 2]
    red = jnp.where(even, f_low, f_high)
    black = jnp.where(even, f_high, f_low)
    mixed = jnp.concatenate([jnp.where(even, high, low), red], axis=2)
    return jnp.concatenate([mixed, jnp.concatenate([black[first : first + 1], black[first + 1 : first + 2]], axis=2)], axis=0)


def coefficient_shapes(*levels):
    shapes = []
    for lv in levels:
        shapes += [struct(4, lv.rows, 128), struct(3, lv.rows, 128)]
    return shapes


def per_device(right_side, guess):
    ib, ia = pair(face(guess, right_side, 58, 1), face(guess, right_side, 0, 0), "gx")
    x, y = call(compact_kernel, (struct(32, 64, 128), struct(16, 64, 128)), [])(guess, right_side)

    up, down = call(rows_kernel, (struct(248, 128), struct(248, 128)), [])(
        ib, ia, guess[:, 0:8], guess[:, 56:64], right_side[:, 0:8], right_side[:, 56:64]
    )
    jb, ja = pair(up, down, "gy")
    xf, yf, ku, kd = call(
        pack_kernel, (struct(40, 80, 128), struct(24, 80, 128), struct(5, 80, 128), struct(5, 80, 128)), []
    )(ib, ia, x, y, jb, ja)
    kb, ka = pair(ku, kd, "gz", True)
    fine = L0.shape()
    field = struct(*fine)
    weights = jax.ShapeDtypeStruct((256, 128), BF16)
    black, g_red, g_black, c0, d0, w0, lanes = call(
        spread_kernel, (field, field, field, *coefficient_shapes(L0), weights, weights), []
    )(xf, yf)
    v0, gr0, gb0, low_quads, high_quads = call(
        fine_kernel,
        (field, field, field, struct(4, 32, 128), struct(4, 32, 128)),
        [fine, fine, fine, (32, 40, 128), (32, 40, 128), (8, 40, 128)],
    )(black, g_red, g_black, kb, ka, c0, d0, w0, lanes)

    ib, ia = pair(high_quads, low_quads, "gx")
    shapes = coefficient_shapes(*WINDOWS, *WHOLES) + [weights, jax.ShapeDtypeStruct((6, 256, 256), BF16)]
    c1, d1, c2, d2, c3o, d3o, c3, _, c4, d4, c5, d5, c6, _, halving, doubling = call(
        geometry_kernel, tuple(shapes), []
    )(low_quads)

    def quad_ends(low):
        return jnp.concatenate([part[:, low : low + 16] for part in (ib, low_quads, high_quads, ia)], axis=0)

    jb, ja = pair(quad_ends(16), quad_ends(0), "gy")
    parts = (ib, ia, low_quads, high_quads, jb, ja)
    ku, kd = call(pack_quads_kernel, (struct(8, 64, 128), struct(8, 64, 128)), [])(*parts)
    kb, ka = pair(ku, kd, "gz", True)
    (qf,) = call(join_kernel, (struct(16, 64, 128),), [])(*parts)
    s1, s2, s3 = L1.shape(), L2.shape(), L3_OWN.shape()
    v1, gr1, gb1, v2, gr2, gb2, message = call(
        middle_kernel,
        tuple(struct(*s) for s in (s1, s1, s1, s2, s2, s2, (64, 5, 1, 128))),
        [s1, s1, (28, 32, 128), (28, 32, 128), s2, s2, (12, 16, 128), (12, 16, 128)]
        + [s3, s3, s3, s3, s3, (4, 8, 128), (4, 8, 128), (8, 16, 128)],
    )(qf, kb, ka, c1, d1, c2, d2, c3o, d3o, halving, lanes)

    tiles = lax.all_to_all(message, ("gy", "gz"), 0, 0)
    message, near = call(
        plane_kernel, (struct(8, 56, 128), struct(8, 24, 128)), [(64, 128), (32, 128), (9, 8, 128)]
    )(tiles)
    tiles = lax.all_to_all(message, "gx", 0, 0)
    s3, s4, s5, s6 = L3.shape(), L4.shape(), L5.shape(), L6.shape()
    return tuple(
        call(
            coarse_kernel,
            (struct(64, 64, 64), struct(64, 64, 64)),
            [s4, s4, s4, s4, s4, (16, 16, 128), (16, 16, 128)]
            + [s5, s5, s5, s5, s5, (8, 8, 128), (8, 8, 128)]
            + [s6, s6, s6, s6, (40, 48, 128)]
            + [s3, s3, s3, s3, s3, s2, s2, s1, s1, fine, fine, fine]
            + [(42, 40, 128), (42, 40, 128), (42, 40, 128), (40, 40, 128), (40, 40, 128), (40, 64, 128), (16, 80, 128), (64, 64, 64), (64, 64, 64)],
            out_space=pl.ANY,
            semaphores=16,
        )(tiles, near, v2, gr2, gb2, v1, gr1, gb1, v0, gr0, gb0, c0, d0, c1, c2, c3, c4, d4, c5, d5, c6, halving, doubling, lanes)
    )


def solution(mesh):
    return jax.shard_map(
        per_device,
        mesh=mesh,
        in_specs=(P("gx", "gy", "gz"), P("gx", "gy", "gz")),
        out_specs=(P("gx", "gy", "gz"), P("gx", "gy", "gz")),
        check_vma=False,
    )
```

profile of v0, /device:TPU:1, one launch (start us, length us, event | category | flops | bytes accessed | tf_op | source)
XLA Modules:
  0.0 118.6 jit_solution(11408023676321408799)
XLA Ops:
  0.7 1.4 %slice_select_fusion = (f32[3,64,64]{2,1,0:T(8,128)S(1)}, f32[3,64,64]{2,1,0:T(8,128)S(1)}, f32[3,64,64]{2,1,0:T(8,128)S(1)}, f32[3,64,64]{2,1,0:T(8,128)S(1)}, ...) fusion(f32[64,64,64]{2,1,0:T(8,128)} %guess.1, pred[64,64]{1,0:T(8,128)(4,1)S(1)} %and_compare_fusion, ...), kind=kLoop, calls=%fused_computation.4 | loop fusion | flops 73728 | bytes 692224 | tf_op jit(solution)/shard_map/jit(_where)/select_n | solution.py:972
  2.2 1.4 %collective-permute-start.1 = (f32[4,64,128]{2,1,0:T(8,128)S(1)}, f32[4,64,128]{2,1,0:T(8,128)S(1)}, u32[]{:S(2)}, u32[]{:S(2)}) collective-permute-start(f32[4,64,128]{2,1,0:T(8,128)S(1)} %maximum_maximum_fusion.1), channel_id=1, source_target_pairs={{64,0},{128,64},{192,128},{256,192},{320,256},{384,320},{448,384},... | collective-permute-start | bytes 393224 | tf_op jit(solution)/shard_map/ppermute | solution.py:961
  3.8 5.5 %collective-permute-start = (f32[4,64,128]{2,1,0:T(8,128)S(1)}, f32[4,64,128]{2,1,0:T(8,128)S(1)}, u32[]{:S(2)}, u32[]{:S(2)}) collective-permute-start(f32[4,64,128]{2,1,0:T(8,128)S(1)} %maximum_maximum_fusion), channel_id=1, source_target_pairs={{0,64},{64,128},{128,192},{192,256},{256,320},{320,384},{384,448},... | collective-permute-start | bytes 393224 | tf_op jit(solution)/shard_map/ppermute | solution.py:962
  9.2 1.1 fusion
  10.4 0.8 collective-permute-done.ib
  11.3 3.4 %collective-permute-start.2 = (f32[248,128]{1,0:T(8,128)S(1)}, f32[248,128]{1,0:T(8,128)S(1)}, u32[]{:S(2)}, u32[]{:S(2)}) collective-permute-start(f32[248,128]{1,0:T(8,128)S(1)} %get-tuple-element.49), channel_id=1, source_target_pairs={{0,8},{8,16},{16,24},{24,32},{32,40},{40,48},{48,56},{1,9},{9,17},... | collective-permute-start | bytes 380936 | tf_op jit(solution)/shard_map/ppermute | solution.py:962
  14.8 1.3 %collective-permute-start.3 = (f32[248,128]{1,0:T(8,128)S(1)}, f32[248,128]{1,0:T(8,128)S(1)}, u32[]{:S(2)}, u32[]{:S(2)}) collective-permute-start(f32[248,128]{1,0:T(8,128)S(1)} %get-tuple-element.50), channel_id=1, source_target_pairs={{8,0},{16,8},{24,16},{32,24},{40,32},{48,40},{56,48},{9,1},{17,9},... | collective-permute-start | bytes 380936 | tf_op jit(solution)/shard_map/ppermute | solution.py:961
  16.1 1.0 shard_map.41
  17.1 3.4 %collective-permute-done.3.ja = f32[248,128]{1,0:T(8,128)S(1)} collective-permute-done((f32[248,128]{1,0:T(8,128)S(1)}, f32[248,128]{1,0:T(8,128)S(1)}, u32[]{:S(2)}, u32[]{:S(2)}) %collective-permute-start.3) | collective-permute-done | bytes 127008 | tf_op jit(solution)/shard_map/ppermute | solution.py:961
  20.4 1.0 shard_map.43
  21.4 4.1 %collective-permute-start.4 = (f32[5,80,128]{2,1,0:T(8,128)S(1)}, f32[5,80,128]{2,1,0:T(8,128)S(1)}, u32[]{:S(2)}, u32[]{:S(2)}) collective-permute-start(f32[5,80,128]{2,1,0:T(8,128)S(1)} %get-tuple-element.56), channel_id=1, source_target_pairs={{0,1},{1,2},{2,3},{3,4},{4,5},{5,6},{6,7},{7,0},{8,9},{9,10},{10,1... | collective-permute-start | bytes 614408 | tf_op jit(solution)/shard_map/ppermute | solution.py:962
  25.5 1.5 %collective-permute-start.5 = (f32[5,80,128]{2,1,0:T(8,128)S(1)}, f32[5,80,128]{2,1,0:T(8,128)S(1)}, u32[]{:S(2)}, u32[]{:S(2)}) collective-permute-start(f32[5,80,128]{2,1,0:T(8,128)S(1)} %get-tuple-element.57), channel_id=1, source_target_pairs={{1,0},{2,1},{3,2},{4,3},{5,4},{6,5},{7,6},{0,7},{9,8},{10,9},{11,1... | collective-permute-start | bytes 614408 | tf_op jit(solution)/shard_map/ppermute | solution.py:961
  27.0 1.7 %shard_map.44 = (f32[42,80,128]{2,1,0:T(8,128)S(1)}, f32[42,80,128]{2,1,0:T(8,128)S(1)}, f32[42,80,128]{2,1,0:T(8,128)S(1)}, f32[4,80,128]{2,1,0:T(8,128)S(1)}, ...) custom-call(f32[40,80,128]{2,1,0:T(8,128)S(1)} %get-tuple-element.51.xf, ...), custom_call_target="tpu_custom_call" | custom-call | flops 2000000 | bytes 1000000 | tf_op jit(solution)/shard_map/pallas_call | solution.py:945
  28.7 2.3 %collective-permute-done.5.ka = f32[5,80,128]{2,1,0:T(8,128)S(1)} collective-permute-done((f32[5,80,128]{2,1,0:T(8,128)S(1)}, f32[5,80,128]{2,1,0:T(8,128)S(1)}, u32[]{:S(2)}, u32[]{:S(2)}) %collective-permute-start.5) | collective-permute-done | bytes 204832 | tf_op jit(solution)/shard_map/ppermute | solution.py:961
  31.0 4.3 %shard_map.45 = (f32[42,80,128]{2,1,0:T(8,128)S(1)}, f32[42,80,128]{2,1,0:T(8,128)S(1)}, f32[42,80,128]{2,1,0:T(8,128)S(1)}, f32[4,32,128]{2,1,0:T(8,128)S(1)}, f32[4,32,128]{2,1,0:T(8,128)S(1)}) custom-call(f32[42,80,128]{2,1,0:T(8,128)S(1)} %get-tuple-element.53.black0, f32[42,80,128]{2,1,0:T(8,128)S(1)} %get-tuple-element.54.g_red0, ...), custom_call_target="tpu_custom_call" | custom-call | flops 2000000 | bytes 1000000 | tf_op jit(solution)/shard_map/pallas_call | solution.py:945
  35.3 4.1 %collective-permute-start.6 = (f32[4,32,128]{2,1,0:T(8,128)S(1)}, f32[4,32,128]{2,1,0:T(8,128)S(1)}, u32[]{:S(2)}, u32[]{:S(2)}) collective-permute-start(f32[4,32,128]{2,1,0:T(8,128)S(1)} %get-tuple-element.62.high_quads), channel_id=1, source_target_pairs={{0,64},{64,128},{128,192},{192,256},{256,320},{320,384},{384,448},... | collective-permute-start | bytes 196616 | tf_op jit(solution)/shard_map/ppermute | solution.py:962
  39.4 1.3 %collective-permute-start.7 = (f32[4,32,128]{2,1,0:T(8,128)S(1)}, f32[4,32,128]{2,1,0:T(8,128)S(1)}, u32[]{:S(2)}, u32[]{:S(2)}) collective-permute-start(f32[4,32,128]{2,1,0:T(8,128)S(1)} %get-tuple-element.63.low_quads.after), channel_id=1, source_target_pairs={{64,0},{128,64},{192,128},{256,192},{320,256},{384,320},{448,384},... | collective-permute-start | bytes 196616 | tf_op jit(solution)/shard_map/ppermute | solution.py:961
  40.8 4.0 %collective-permute-done.7.ia = f32[4,32,128]{2,1,0:T(8,128)S(1)} collective-permute-done((f32[4,32,128]{2,1,0:T(8,128)S(1)}, f32[4,32,128]{2,1,0:T(8,128)S(1)}, u32[]{:S(2)}, u32[]{:S(2)}) %collective-permute-start.7) | collective-permute-done | bytes 65568 | tf_op jit(solution)/shard_map/ppermute | solution.py:961
  44.8 3.2 %collective-permute-start.8 = (f32[16,16,128]{2,1,0:T(8,128)S(1)}, f32[16,16,128]{2,1,0:T(8,128)S(1)}, u32[]{:S(2)}, u32[]{:S(2)}) collective-permute-start(f32[16,16,128]{2,1,0:T(8,128)S(1)} %pad_maximum_fusion), channel_id=1, source_target_pairs={{0,8},{8,16},{16,24},{24,32},{32,40},{40,48},{48,56},{1,9},{9,17},... | collective-permute-start | bytes 393224 | tf_op jit(solution)/shard_map/ppermute | solution.py:962
  48.0 1.3 %collective-permute-start.9 = (f32[16,16,128]{2,1,0:T(8,128)S(1)}, f32[16,16,128]{2,1,0:T(8,128)S(1)}, u32[]{:S(2)}, u32[]{:S(2)}) collective-permute-start(f32[16,16,128]{2,1,0:T(8,128)S(1)} %pad_maximum_fusion.1), channel_id=1, source_target_pairs={{8,0},{16,8},{24,16},{32,24},{40,32},{48,40},{56,48},{9,1},{17,9},... | collective-permute-start | bytes 393224 | tf_op jit(solution)/shard_map/ppermute | solution.py:961
  49.3 0.6 collective-permute-done.8.jb
  49.9 4.8 %collective-permute-done.9.ja = f32[16,16,128]{2,1,0:T(8,128)S(1)} collective-permute-done((f32[16,16,128]{2,1,0:T(8,128)S(1)}, f32[16,16,128]{2,1,0:T(8,128)S(1)}, u32[]{:S(2)}, u32[]{:S(2)}) %collective-permute-start.9) | collective-permute-done | bytes 131104 | tf_op jit(solution)/shard_map/ppermute | solution.py:961
  54.8 0.9 shard_map.47
  55.7 2.9 %collective-permute-start.10 = (f32[8,64,128]{2,1,0:T(8,128)S(1)}, f32[8,64,128]{2,1,0:T(8,128)S(1)}, u32[]{:S(2)}, u32[]{:S(2)}) collective-permute-start(f32[8,64,128]{2,1,0:T(8,128)S(1)} %get-tuple-element.64), channel_id=1, source_target_pairs={{0,1},{1,2},{2,3},{3,4},{4,5},{5,6},{6,7},{7,0},{8,9},{9,10},{10,1... | collective-permute-start | bytes 786440 | tf_op jit(solution)/shard_map/ppermute | solution.py:962
  58.5 0.8 shard_map.48
  59.3 2.5 %collective-permute-done.10.kb = f32[8,64,128]{2,1,0:T(8,128)S(1)} collective-permute-done((f32[8,64,128]{2,1,0:T(8,128)S(1)}, f32[8,64,128]{2,1,0:T(8,128)S(1)}, u32[]{:S(2)}, u32[]{:S(2)}) %collective-permute-start.10) | collective-permute-done | bytes 262176 | tf_op jit(solution)/shard_map/ppermute | solution.py:962
  61.8 2.6 %collective-permute-done.11.ka = f32[8,64,128]{2,1,0:T(8,128)S(1)} collective-permute-done((f32[8,64,128]{2,1,0:T(8,128)S(1)}, f32[8,64,128]{2,1,0:T(8,128)S(1)}, u32[]{:S(2)}, u32[]{:S(2)}) %collective-permute-start.11) | collective-permute-done | bytes 262176 | tf_op jit(solution)/shard_map/ppermute | solution.py:961
  64.4 3.0 %shard_map.49 = (f32[32,64,128]{2,1,0:T(8,128)S(1)}, f32[32,64,128]{2,1,0:T(8,128)S(1)}, f32[32,64,128]{2,1,0:T(8,128)S(1)}, f32[16,32,128]{2,1,0:T(8,128)S(1)},...) custom-call(f32[16,64,128]{2,1,0:T(8,128)S(1)} %shard_map.46.qf, ...), custom_call_target="tpu_custom_call" | custom-call | flops 2000000 | bytes 1000000 | tf_op jit(solution)/shard_map/pallas_call | solution.py:945
  67.4 21.4 %all_to_all.10.tiles = f32[64,5,1,128]{3,2,1,0:T(1,128)S(1)} all-to-all(f32[64,5,1,128]{3,2,1,0:T(1,128)S(1)} %get-tuple-element.73), channel_id=1, replica_groups=mesh['gx'=8,'gy'=8,'gz'=8] {'gy','gz'}, dimensions={0} | all-to-all | bytes 327680 | tf_op jit(solution)/shard_map/all_to_all | solution.py:1029
  88.8 0.4 shard_map.50
  89.2 20.1 %all_to_all.11.tiles = f32[8,56,128]{2,1,0:T(8,128)S(1)} all-to-all(f32[8,56,128]{2,1,0:T(8,128)S(1)} %get-tuple-element.74), channel_id=1, replica_groups=mesh['gx'=8,'gy'=8,'gz'=8] {'gx'}, dimensions={0} | all-to-all | bytes 458752 | tf_op jit(solution)/shard_map/all_to_all | solution.py:1033
  109.3 9.1 %shard_map.51 = (f32[64,64,64]{2,1,0:T(8,128)}, f32[64,64,64]{2,1,0:T(8,128)}) custom-call(f32[8,56,128]{2,1,0:T(8,128)S(1)} %all_to_all.11.tiles, f32[8,24,128]{2,1,0:T(8,128)S(1)} %get-tuple-element.75.near, f32[16,32,128]{2,1,0:T(8,128)S(1)} %get-tuple-element.76.v2, f32[16,32,128]{2,1,0:T(8,128)S(1)} %get-tuple-element.77.gr2, ...), custom_call_target="tpu_custom_call" | custom-call | flops 2000000 | bytes 1000000 | tf_op jit(solution)/shard_map/pallas_call | solution.py:945
  (22 shorter events, 0.5 us)
Async XLA Ops:
  0.6 8.6 %copy-start = (f32[64,64,64]{2,1,0:T(8,128)S(1)}, f32[64,64,64]{2,1,0:T(8,128)}, u32[]{:S(2)}) copy-start(f32[64,64,64]{2,1,0:T(8,128)} %guess.1) | copy-start | bytes 3145732
  2.1 14.0 %copy-start.1 = (f32[64,64,64]{2,1,0:T(8,128)S(1)}, f32[64,64,64]{2,1,0:T(8,128)}, u32[]{:S(2)}) copy-start(f32[64,64,64]{2,1,0:T(8,128)} %source.1) | copy-start | bytes 3145732
  2.2 8.1 %collective-permute-start.1 = (f32[4,64,128]{2,1,0:T(8,128)S(1)}, f32[4,64,128]{2,1,0:T(8,128)S(1)}, u32[]{:S(2)}, u32[]{:S(2)}) collective-permute-start(f32[4,64,128]{2,1,0:T(8,128)S(1)} %maximum_maximum_fusion.1), channel_id=1, source_target_pairs={{64,0},{128,64},{192,128},{256,192},{320,256},{384,320},{448,384},... | collective-permute-start | bytes 393224 | tf_op jit(solution)/shard_map/ppermute | solution.py:961
  3.8 7.4 %collective-permute-start = (f32[4,64,128]{2,1,0:T(8,128)S(1)}, f32[4,64,128]{2,1,0:T(8,128)S(1)}, u32[]{:S(2)}, u32[]{:S(2)}) collective-permute-start(f32[4,64,128]{2,1,0:T(8,128)S(1)} %maximum_maximum_fusion), channel_id=1, source_target_pairs={{0,64},{64,128},{128,192},{192,256},{256,320},{320,384},{384,448},... | collective-permute-start | bytes 393224 | tf_op jit(solution)/shard_map/ppermute | solution.py:962
  11.3 5.7 %collective-permute-start.2 = (f32[248,128]{1,0:T(8,128)S(1)}, f32[248,128]{1,0:T(8,128)S(1)}, u32[]{:S(2)}, u32[]{:S(2)}) collective-permute-start(f32[248,128]{1,0:T(8,128)S(1)} %get-tuple-element.49), channel_id=1, source_target_pairs={{0,8},{8,16},{16,24},{24,32},{32,40},{40,48},{48,56},{1,9},{9,17},... | collective-permute-start | bytes 380936 | tf_op jit(solution)/shard_map/ppermute | solution.py:962
  14.8 5.7 %collective-permute-start.3 = (f32[248,128]{1,0:T(8,128)S(1)}, f32[248,128]{1,0:T(8,128)S(1)}, u32[]{:S(2)}, u32[]{:S(2)}) collective-permute-start(f32[248,128]{1,0:T(8,128)S(1)} %get-tuple-element.50), channel_id=1, source_target_pairs={{8,0},{16,8},{24,16},{32,24},{40,32},{48,40},{56,48},{9,1},{17,9},... | collective-permute-start | bytes 380936 | tf_op jit(solution)/shard_map/ppermute | solution.py:961
  21.4 7.3 %collective-permute-start.4 = (f32[5,80,128]{2,1,0:T(8,128)S(1)}, f32[5,80,128]{2,1,0:T(8,128)S(1)}, u32[]{:S(2)}, u32[]{:S(2)}) collective-permute-start(f32[5,80,128]{2,1,0:T(8,128)S(1)} %get-tuple-element.56), channel_id=1, source_target_pairs={{0,1},{1,2},{2,3},{3,4},{4,5},{5,6},{6,7},{7,0},{8,9},{9,10},{10,1... | collective-permute-start | bytes 614408 | tf_op jit(solution)/shard_map/ppermute | solution.py:962
  25.5 5.5 %collective-permute-start.5 = (f32[5,80,128]{2,1,0:T(8,128)S(1)}, f32[5,80,128]{2,1,0:T(8,128)S(1)}, u32[]{:S(2)}, u32[]{:S(2)}) collective-permute-start(f32[5,80,128]{2,1,0:T(8,128)S(1)} %get-tuple-element.57), channel_id=1, source_target_pairs={{1,0},{2,1},{3,2},{4,3},{5,4},{6,5},{7,6},{0,7},{9,8},{10,9},{11,1... | collective-permute-start | bytes 614408 | tf_op jit(solution)/shard_map/ppermute | solution.py:961
  35.3 5.4 %collective-permute-start.6 = (f32[4,32,128]{2,1,0:T(8,128)S(1)}, f32[4,32,128]{2,1,0:T(8,128)S(1)}, u32[]{:S(2)}, u32[]{:S(2)}) collective-permute-start(f32[4,32,128]{2,1,0:T(8,128)S(1)} %get-tuple-element.62.high_quads), channel_id=1, source_target_pairs={{0,64},{64,128},{128,192},{192,256},{256,320},{320,384},{384,448},... | collective-permute-start | bytes 196616 | tf_op jit(solution)/shard_map/ppermute | solution.py:962
  39.4 5.4 %collective-permute-start.7 = (f32[4,32,128]{2,1,0:T(8,128)S(1)}, f32[4,32,128]{2,1,0:T(8,128)S(1)}, u32[]{:S(2)}, u32[]{:S(2)}) collective-permute-start(f32[4,32,128]{2,1,0:T(8,128)S(1)} %get-tuple-element.63.low_quads.after), channel_id=1, source_target_pairs={{64,0},{128,64},{192,128},{256,192},{320,256},{384,320},{448,384},... | collective-permute-start | bytes 196616 | tf_op jit(solution)/shard_map/ppermute | solution.py:961
  44.8 5.1 %collective-permute-start.8 = (f32[16,16,128]{2,1,0:T(8,128)S(1)}, f32[16,16,128]{2,1,0:T(8,128)S(1)}, u32[]{:S(2)}, u32[]{:S(2)}) collective-permute-start(f32[16,16,128]{2,1,0:T(8,128)S(1)} %pad_maximum_fusion), channel_id=1, source_target_pairs={{0,8},{8,16},{16,24},{24,32},{32,40},{40,48},{48,56},{1,9},{9,17},... | collective-permute-start | bytes 393224 | tf_op jit(solution)/shard_map/ppermute | solution.py:962
  48.0 6.7 %collective-permute-start.9 = (f32[16,16,128]{2,1,0:T(8,128)S(1)}, f32[16,16,128]{2,1,0:T(8,128)S(1)}, u32[]{:S(2)}, u32[]{:S(2)}) collective-permute-start(f32[16,16,128]{2,1,0:T(8,128)S(1)} %pad_maximum_fusion.1), channel_id=1, source_target_pairs={{8,0},{16,8},{24,16},{32,24},{40,32},{48,40},{56,48},{9,1},{17,9},... | collective-permute-start | bytes 393224 | tf_op jit(solution)/shard_map/ppermute | solution.py:961
  55.7 6.2 %collective-permute-start.10 = (f32[8,64,128]{2,1,0:T(8,128)S(1)}, f32[8,64,128]{2,1,0:T(8,128)S(1)}, u32[]{:S(2)}, u32[]{:S(2)}) collective-permute-start(f32[8,64,128]{2,1,0:T(8,128)S(1)} %get-tuple-element.64), channel_id=1, source_target_pairs={{0,1},{1,2},{2,3},{3,4},{4,5},{5,6},{6,7},{7,0},{8,9},{9,10},{10,1... | collective-permute-start | bytes 786440 | tf_op jit(solution)/shard_map/ppermute | solution.py:962
  58.5 5.9 %collective-permute-start.11 = (f32[8,64,128]{2,1,0:T(8,128)S(1)}, f32[8,64,128]{2,1,0:T(8,128)S(1)}, u32[]{:S(2)}, u32[]{:S(2)}) collective-permute-start(f32[8,64,128]{2,1,0:T(8,128)S(1)} %get-tuple-element.65), channel_id=1, source_target_pairs={{1,0},{2,1},{3,2},{4,3},{5,4},{6,5},{7,6},{0,7},{9,8},{10,9},{11,1... | collective-permute-start | bytes 786440 | tf_op jit(solution)/shard_map/ppermute | solution.py:961
where the time goes:
time: 119 us
  blocking collectives  41.5 us (35%)
  starting transfers between devices  29.9 us (25%)
  Pallas kernels  22.3 us (19%)
  waiting for transfers between devices  21 us (18%)
  other arithmetic  1.65 us (1%)
    ppermute x6, starting transfers between devices, pair(): before = lax.ppermute(to_next, axis, up)  23.1 us
    pallas_call x11, Pallas kernels, run(): pl.pallas_call(kernel, out_shape=outs, in_specs=[space] * len(args), out_...  22.3 us
    all_to_all x1, blocking collectives, per_device(): tiles = lax.all_to_all(message, ('gy', 'gz'), 0, 0)  21.4 us
    all_to_all x1, blocking collectives, per_device(): tiles = lax.all_to_all(message, 'gx', 0, 0)  20.1 us
    ppermute x6, waiting for transfers between devices, pair(): after = lax.ppermute(to_before, axis, down)  17.1 us
    ppermute x6, starting transfers between devices, pair(): after = lax.ppermute(to_before, axis, down)  6.79 us
    ppermute x6, waiting for transfers between devices, pair(): before = lax.ppermute(to_next, axis, up)  3.92 us
  transfers between devices with their start and end apart: 12, of which 8 were waited for; matrix products, arithmetic and copies ran while one was open for 1% of the time, Pallas kernels for 3%

commit v1 on v0

--- a/solution.py
+++ b/solution.py
@@ -514,7 +514,7 @@
 
 def fine_kernel(
     black0, g_red0, g_black0, kb, ka, c_ref, d_ref, weights, lanes, v_black, g_red, g_black, low_quads, high_quads,
-    black, red, rest, z_ref, planes, natural,
+    black, red, rest, z_ref, planes, natural, later,
 ):
     edges = block_edges()
     zero = jnp.zeros((80, 128), F32)
@@ -536,8 +536,8 @@
         g_red[p + 1] = g_red0[p + 1] + turn(edge, -turned, 1)
 
     def merge_black(n):
-        below, above = sides(n // 8)
-        below = turn(below, 2, 1)
+        above = jnp.where(edges.khi, 0.0, gather_rows(ka, n // 8, 80))
+        below = later[n // 8]
         turned = 8 * (n % 8)
         place = (lane - turned) & 127
         edge = jnp.where((place >= 5) & (place < 8), above, jnp.where((place >= 66) & (place < 69), below, 0.0))
@@ -545,6 +545,8 @@
         edge = jnp.where((place >= 69) & (place < 72), above, jnp.where((place >= 2) & (place < 5), below, 0.0))
         g_black[2 * n + 3] = g_black0[2 * n + 3] + turn(edge, -5 - turned, 1)
 
+    for u in range(3):
+        later[u] = turn(sides(u)[0], 2, 1)
     for q in (0, 1, 38, 39, 40, 41):
         g_black[q] = zero
     for ref in (black, g_red):
@@ -587,8 +589,8 @@
     low_half = (lanes_of((64, 128)) & 31) < 16
     for u in range(8):
         first, second = (quad_rows(ib, ia, low_quads, high_quads, jb, ja, 2 * u + k) for k in range(2))
-        kd[u] = turn(jnp.where(low_half, first, turn(second, 16, 1)), 32, 1)
-        ku[u] = turn(jnp.where(low_half, turn(first, -16, 1), second), -32, 1)
+        kd[u] = jnp.where(low_half, turn(first, 32, 1), turn(second, 48, 1))
+        ku[u] = jnp.where(low_half, turn(first, -48, 1), turn(second, -32, 1))
 
 
 def join_kernel(ib, ia, low_quads, high_quads, jb, ja, qf):
@@ -1001,7 +1003,7 @@
     v0, gr0, gb0, low_quads, high_quads = call(
         fine_kernel,
         (field, field, field, struct(4, 32, 128), struct(4, 32, 128)),
-        [fine, fine, fine, (32, 40, 128), (32, 40, 128), (8, 40, 128)],
+        [fine, fine, fine, (32, 40, 128), (32, 40, 128), (8, 40, 128), (3, 80, 128)],
     )(black, g_red, g_black, kb, ka, c0, d0, w0, lanes)
 
     ib, ia = pair(high_quads, low_quads, "gx")

time: 119 us -> 118 us (level)
  no operation moved by 1% of the time
where the time goes in v1:
time: 118 us
  blocking collectives  41.5 us (35%)
  starting transfers between devices  29.9 us (25%)
  Pallas kernels  21.6 us (18%)
  waiting for transfers between devices  21 us (18%)
  other arithmetic  1.65 us (1%)
    ppermute x6, starting transfers between devices, pair(): before = lax.ppermute(to_next, axis, up)  23.1 us
    pallas_call x11, Pallas kernels, run(): pl.pallas_call(kernel, out_shape=outs, in_specs=[space] * len(args), out_...  21.6 us
    all_to_all x1, blocking collectives, per_device(): tiles = lax.all_to_all(message, ('gy', 'gz'), 0, 0)  21.4 us
    all_to_all x1, blocking collectives, per_device(): tiles = lax.all_to_all(message, 'gx', 0, 0)  20.1 us
    ppermute x6, waiting for transfers between devices, pair(): after = lax.ppermute(to_before, axis, down)  17.1 us
    ppermute x6, starting transfers between devices, pair(): after = lax.ppermute(to_before, axis, down)  6.79 us
    ppermute x6, waiting for transfers between devices, pair(): before = lax.ppermute(to_next, axis, up)  3.92 us
  transfers between devices with their start and end apart: 12, of which 8 were waited for; matrix products, arithmetic and copies ran while one was open for 1% of the time, Pallas kernels for 3%

profile of v1, /device:TPU:1, one launch (start us, length us, event | category | flops | bytes accessed | tf_op | source)
XLA Modules:
  0.0 117.9 jit_solution(12470264534464342832)
XLA Ops:
  0.7 1.4 %slice_select_fusion = (f32[3,64,64]{2,1,0:T(8,128)S(1)}, f32[3,64,64]{2,1,0:T(8,128)S(1)}, f32[3,64,64]{2,1,0:T(8,128)S(1)}, f32[3,64,64]{2,1,0:T(8,128)S(1)}, ...) fusion(f32[64,64,64]{2,1,0:T(8,128)} %guess.1, pred[64,64]{1,0:T(8,128)(4,1)S(1)} %and_compare_fusion, ...), kind=kLoop, calls=%fused_computation.4 | loop fusion | flops 73728 | bytes 692224 | tf_op jit(solution)/shard_map/jit(_where)/select_n | solution.py:974
  2.2 1.4 %collective-permute-start.1 = (f32[4,64,128]{2,1,0:T(8,128)S(1)}, f32[4,64,128]{2,1,0:T(8,128)S(1)}, u32[]{:S(2)}, u32[]{:S(2)}) collective-permute-start(f32[4,64,128]{2,1,0:T(8,128)S(1)} %maximum_maximum_fusion.1), channel_id=1, source_target_pairs={{64,0},{128,64},{192,128},{256,192},{320,256},{384,320},{448,384},... | collective-permute-start | bytes 393224 | tf_op jit(solution)/shard_map/ppermute | solution.py:963
  3.8 5.5 %collective-permute-start = (f32[4,64,128]{2,1,0:T(8,128)S(1)}, f32[4,64,128]{2,1,0:T(8,128)S(1)}, u32[]{:S(2)}, u32[]{:S(2)}) collective-permute-start(f32[4,64,128]{2,1,0:T(8,128)S(1)} %maximum_maximum_fusion), channel_id=1, source_target_pairs={{0,64},{64,128},{128,192},{192,256},{256,320},{320,384},{384,448},... | collective-permute-start | bytes 393224 | tf_op jit(solution)/shard_map/ppermute | solution.py:964
  9.2 1.1 fusion
  10.4 0.8 collective-permute-done.ib
  11.3 3.4 %collective-permute-start.2 = (f32[248,128]{1,0:T(8,128)S(1)}, f32[248,128]{1,0:T(8,128)S(1)}, u32[]{:S(2)}, u32[]{:S(2)}) collective-permute-start(f32[248,128]{1,0:T(8,128)S(1)} %get-tuple-element.49), channel_id=1, source_target_pairs={{0,8},{8,16},{16,24},{24,32},{32,40},{40,48},{48,56},{1,9},{9,17},... | collective-permute-start | bytes 380936 | tf_op jit(solution)/shard_map/ppermute | solution.py:964
  14.8 1.3 %collective-permute-start.3 = (f32[248,128]{1,0:T(8,128)S(1)}, f32[248,128]{1,0:T(8,128)S(1)}, u32[]{:S(2)}, u32[]{:S(2)}) collective-permute-start(f32[248,128]{1,0:T(8,128)S(1)} %get-tuple-element.50), channel_id=1, source_target_pairs={{8,0},{16,8},{24,16},{32,24},{40,32},{48,40},{56,48},{9,1},{17,9},... | collective-permute-start | bytes 380936 | tf_op jit(solution)/shard_map/ppermute | solution.py:963
  16.1 1.0 shard_map.41
  17.1 3.4 %collective-permute-done.3.ja = f32[248,128]{1,0:T(8,128)S(1)} collective-permute-done((f32[248,128]{1,0:T(8,128)S(1)}, f32[248,128]{1,0:T(8,128)S(1)}, u32[]{:S(2)}, u32[]{:S(2)}) %collective-permute-start.3) | collective-permute-done | bytes 127008 | tf_op jit(solution)/shard_map/ppermute | solution.py:963
  20.4 1.0 shard_map.43
  21.4 4.1 %collective-permute-start.4 = (f32[5,80,128]{2,1,0:T(8,128)S(1)}, f32[5,80,128]{2,1,0:T(8,128)S(1)}, u32[]{:S(2)}, u32[]{:S(2)}) collective-permute-start(f32[5,80,128]{2,1,0:T(8,128)S(1)} %get-tuple-element.56), channel_id=1, source_target_pairs={{0,1},{1,2},{2,3},{3,4},{4,5},{5,6},{6,7},{7,0},{8,9},{9,10},{10,1... | collective-permute-start | bytes 614408 | tf_op jit(solution)/shard_map/ppermute | solution.py:964
  25.5 1.5 %collective-permute-start.5 = (f32[5,80,128]{2,1,0:T(8,128)S(1)}, f32[5,80,128]{2,1,0:T(8,128)S(1)}, u32[]{:S(2)}, u32[]{:S(2)}) collective-permute-start(f32[5,80,128]{2,1,0:T(8,128)S(1)} %get-tuple-element.57), channel_id=1, source_target_pairs={{1,0},{2,1},{3,2},{4,3},{5,4},{6,5},{7,6},{0,7},{9,8},{10,9},{11,1... | collective-permute-start | bytes 614408 | tf_op jit(solution)/shard_map/ppermute | solution.py:963
  27.0 1.7 %shard_map.44 = (f32[42,80,128]{2,1,0:T(8,128)S(1)}, f32[42,80,128]{2,1,0:T(8,128)S(1)}, f32[42,80,128]{2,1,0:T(8,128)S(1)}, f32[4,80,128]{2,1,0:T(8,128)S(1)}, ...) custom-call(f32[40,80,128]{2,1,0:T(8,128)S(1)} %get-tuple-element.51.xf, ...), custom_call_target="tpu_custom_call" | custom-call | flops 2000000 | bytes 1000000 | tf_op jit(solution)/shard_map/pallas_call | solution.py:947
  28.7 2.3 %collective-permute-done.5.ka = f32[5,80,128]{2,1,0:T(8,128)S(1)} collective-permute-done((f32[5,80,128]{2,1,0:T(8,128)S(1)}, f32[5,80,128]{2,1,0:T(8,128)S(1)}, u32[]{:S(2)}, u32[]{:S(2)}) %collective-permute-start.5) | collective-permute-done | bytes 204832 | tf_op jit(solution)/shard_map/ppermute | solution.py:963
  31.0 4.0 %shard_map.45 = (f32[42,80,128]{2,1,0:T(8,128)S(1)}, f32[42,80,128]{2,1,0:T(8,128)S(1)}, f32[42,80,128]{2,1,0:T(8,128)S(1)}, f32[4,32,128]{2,1,0:T(8,128)S(1)}, f32[4,32,128]{2,1,0:T(8,128)S(1)}) custom-call(f32[42,80,128]{2,1,0:T(8,128)S(1)} %get-tuple-element.53.black0, f32[42,80,128]{2,1,0:T(8,128)S(1)} %get-tuple-element.54.g_red0, ...), custom_call_target="tpu_custom_call" | custom-call | flops 2000000 | bytes 1000000 | tf_op jit(solution)/shard_map/pallas_call | solution.py:947
  35.0 4.1 %collective-permute-start.6 = (f32[4,32,128]{2,1,0:T(8,128)S(1)}, f32[4,32,128]{2,1,0:T(8,128)S(1)}, u32[]{:S(2)}, u32[]{:S(2)}) collective-permute-start(f32[4,32,128]{2,1,0:T(8,128)S(1)} %get-tuple-element.62.high_quads), channel_id=1, source_target_pairs={{0,64},{64,128},{128,192},{192,256},{256,320},{320,384},{384,448},... | collective-permute-start | bytes 196616 | tf_op jit(solution)/shard_map/ppermute | solution.py:964
  39.1 1.3 %collective-permute-start.7 = (f32[4,32,128]{2,1,0:T(8,128)S(1)}, f32[4,32,128]{2,1,0:T(8,128)S(1)}, u32[]{:S(2)}, u32[]{:S(2)}) collective-permute-start(f32[4,32,128]{2,1,0:T(8,128)S(1)} %get-tuple-element.63.low_quads.after), channel_id=1, source_target_pairs={{64,0},{128,64},{192,128},{256,192},{320,256},{384,320},{448,384},... | collective-permute-start | bytes 196616 | tf_op jit(solution)/shard_map/ppermute | solution.py:963
  40.4 4.0 %collective-permute-done.7.ia = f32[4,32,128]{2,1,0:T(8,128)S(1)} collective-permute-done((f32[4,32,128]{2,1,0:T(8,128)S(1)}, f32[4,32,128]{2,1,0:T(8,128)S(1)}, u32[]{:S(2)}, u32[]{:S(2)}) %collective-permute-start.7) | collective-permute-done | bytes 65568 | tf_op jit(solution)/shard_map/ppermute | solution.py:963
  44.5 3.2 %collective-permute-start.8 = (f32[16,16,128]{2,1,0:T(8,128)S(1)}, f32[16,16,128]{2,1,0:T(8,128)S(1)}, u32[]{:S(2)}, u32[]{:S(2)}) collective-permute-start(f32[16,16,128]{2,1,0:T(8,128)S(1)} %pad_maximum_fusion), channel_id=1, source_target_pairs={{0,8},{8,16},{16,24},{24,32},{32,40},{40,48},{48,56},{1,9},{9,17},... | collective-permute-start | bytes 393224 | tf_op jit(solution)/shard_map/ppermute | solution.py:964
  47.7 1.3 %collective-permute-start.9 = (f32[16,16,128]{2,1,0:T(8,128)S(1)}, f32[16,16,128]{2,1,0:T(8,128)S(1)}, u32[]{:S(2)}, u32[]{:S(2)}) collective-permute-start(f32[16,16,128]{2,1,0:T(8,128)S(1)} %pad_maximum_fusion.1), channel_id=1, source_target_pairs={{8,0},{16,8},{24,16},{32,24},{40,32},{48,40},{56,48},{9,1},{17,9},... | collective-permute-start | bytes 393224 | tf_op jit(solution)/shard_map/ppermute | solution.py:963
  49.0 0.6 collective-permute-done.8.jb
  49.6 4.8 %collective-permute-done.9.ja = f32[16,16,128]{2,1,0:T(8,128)S(1)} collective-permute-done((f32[16,16,128]{2,1,0:T(8,128)S(1)}, f32[16,16,128]{2,1,0:T(8,128)S(1)}, u32[]{:S(2)}, u32[]{:S(2)}) %collective-permute-start.9) | collective-permute-done | bytes 131104 | tf_op jit(solution)/shard_map/ppermute | solution.py:963
  54.5 0.3 shard_map.47
  54.8 2.9 %collective-permute-start.10 = (f32[8,64,128]{2,1,0:T(8,128)S(1)}, f32[8,64,128]{2,1,0:T(8,128)S(1)}, u32[]{:S(2)}, u32[]{:S(2)}) collective-permute-start(f32[8,64,128]{2,1,0:T(8,128)S(1)} %get-tuple-element.64), channel_id=1, source_target_pairs={{0,1},{1,2},{2,3},{3,4},{4,5},{5,6},{6,7},{7,0},{8,9},{9,10},{10,1... | collective-permute-start | bytes 786440 | tf_op jit(solution)/shard_map/ppermute | solution.py:964
  57.7 0.8 shard_map.48
  58.5 2.5 %collective-permute-done.10.kb = f32[8,64,128]{2,1,0:T(8,128)S(1)} collective-permute-done((f32[8,64,128]{2,1,0:T(8,128)S(1)}, f32[8,64,128]{2,1,0:T(8,128)S(1)}, u32[]{:S(2)}, u32[]{:S(2)}) %collective-permute-start.10) | collective-permute-done | bytes 262176 | tf_op jit(solution)/shard_map/ppermute | solution.py:964
  61.0 2.6 %collective-permute-done.11.ka = f32[8,64,128]{2,1,0:T(8,128)S(1)} collective-permute-done((f32[8,64,128]{2,1,0:T(8,128)S(1)}, f32[8,64,128]{2,1,0:T(8,128)S(1)}, u32[]{:S(2)}, u32[]{:S(2)}) %collective-permute-start.11) | collective-permute-done | bytes 262176 | tf_op jit(solution)/shard_map/ppermute | solution.py:963
  63.6 3.0 %shard_map.49 = (f32[32,64,128]{2,1,0:T(8,128)S(1)}, f32[32,64,128]{2,1,0:T(8,128)S(1)}, f32[32,64,128]{2,1,0:T(8,128)S(1)}, f32[16,32,128]{2,1,0:T(8,128)S(1)},...) custom-call(f32[16,64,128]{2,1,0:T(8,128)S(1)} %shard_map.46.qf, ...), custom_call_target="tpu_custom_call" | custom-call | flops 2000000 | bytes 1000000 | tf_op jit(solution)/shard_map/pallas_call | solution.py:947
  66.6 21.4 %all_to_all.10.tiles = f32[64,5,1,128]{3,2,1,0:T(1,128)S(1)} all-to-all(f32[64,5,1,128]{3,2,1,0:T(1,128)S(1)} %get-tuple-element.73), channel_id=1, replica_groups=mesh['gx'=8,'gy'=8,'gz'=8] {'gy','gz'}, dimensions={0} | all-to-all | bytes 327680 | tf_op jit(solution)/shard_map/all_to_all | solution.py:1031
  88.0 0.4 shard_map.50
  88.4 20.1 %all_to_all.11.tiles = f32[8,56,128]{2,1,0:T(8,128)S(1)} all-to-all(f32[8,56,128]{2,1,0:T(8,128)S(1)} %get-tuple-element.74), channel_id=1, replica_groups=mesh['gx'=8,'gy'=8,'gz'=8] {'gx'}, dimensions={0} | all-to-all | bytes 458752 | tf_op jit(solution)/shard_map/all_to_all | solution.py:1035
  108.4 9.3 %shard_map.51 = (f32[64,64,64]{2,1,0:T(8,128)}, f32[64,64,64]{2,1,0:T(8,128)}) custom-call(f32[8,56,128]{2,1,0:T(8,128)S(1)} %all_to_all.11.tiles, f32[8,24,128]{2,1,0:T(8,128)S(1)} %get-tuple-element.75.near, f32[16,32,128]{2,1,0:T(8,128)S(1)} %get-tuple-element.76.v2, f32[16,32,128]{2,1,0:T(8,128)S(1)} %get-tuple-element.77.gr2, ...), custom_call_target="tpu_custom_call" | custom-call | flops 2000000 | bytes 1000000 | tf_op jit(solution)/shard_map/pallas_call | solution.py:947
  (22 shorter events, 0.5 us)
Async XLA Ops:
  0.6 8.6 %copy-start = (f32[64,64,64]{2,1,0:T(8,128)S(1)}, f32[64,64,64]{2,1,0:T(8,128)}, u32[]{:S(2)}) copy-start(f32[64,64,64]{2,1,0:T(8,128)} %guess.1) | copy-start | bytes 3145732
  2.1 14.0 %copy-start.1 = (f32[64,64,64]{2,1,0:T(8,128)S(1)}, f32[64,64,64]{2,1,0:T(8,128)}, u32[]{:S(2)}) copy-start(f32[64,64,64]{2,1,0:T(8,128)} %source.1) | copy-start | bytes 3145732
  2.2 8.1 %collective-permute-start.1 = (f32[4,64,128]{2,1,0:T(8,128)S(1)}, f32[4,64,128]{2,1,0:T(8,128)S(1)}, u32[]{:S(2)}, u32[]{:S(2)}) collective-permute-start(f32[4,64,128]{2,1,0:T(8,128)S(1)} %maximum_maximum_fusion.1), channel_id=1, source_target_pairs={{64,0},{128,64},{192,128},{256,192},{320,256},{384,320},{448,384},... | collective-permute-start | bytes 393224 | tf_op jit(solution)/shard_map/ppermute | solution.py:963
  3.8 7.4 %collective-permute-start = (f32[4,64,128]{2,1,0:T(8,128)S(1)}, f32[4,64,128]{2,1,0:T(8,128)S(1)}, u32[]{:S(2)}, u32[]{:S(2)}) collective-permute-start(f32[4,64,128]{2,1,0:T(8,128)S(1)} %maximum_maximum_fusion), channel_id=1, source_target_pairs={{0,64},{64,128},{128,192},{192,256},{256,320},{320,384},{384,448},... | collective-permute-start | bytes 393224 | tf_op jit(solution)/shard_map/ppermute | solution.py:964
  11.3 5.7 %collective-permute-start.2 = (f32[248,128]{1,0:T(8,128)S(1)}, f32[248,128]{1,0:T(8,128)S(1)}, u32[]{:S(2)}, u32[]{:S(2)}) collective-permute-start(f32[248,128]{1,0:T(8,128)S(1)} %get-tuple-element.49), channel_id=1, source_target_pairs={{0,8},{8,16},{16,24},{24,32},{32,40},{40,48},{48,56},{1,9},{9,17},... | collective-permute-start | bytes 380936 | tf_op jit(solution)/shard_map/ppermute | solution.py:964
  14.8 5.7 %collective-permute-start.3 = (f32[248,128]{1,0:T(8,128)S(1)}, f32[248,128]{1,0:T(8,128)S(1)}, u32[]{:S(2)}, u32[]{:S(2)}) collective-permute-start(f32[248,128]{1,0:T(8,128)S(1)} %get-tuple-element.50), channel_id=1, source_target_pairs={{8,0},{16,8},{24,16},{32,24},{40,32},{48,40},{56,48},{9,1},{17,9},... | collective-permute-start | bytes 380936 | tf_op jit(solution)/shard_map/ppermute | solution.py:963
  21.4 7.3 %collective-permute-start.4 = (f32[5,80,128]{2,1,0:T(8,128)S(1)}, f32[5,80,128]{2,1,0:T(8,128)S(1)}, u32[]{:S(2)}, u32[]{:S(2)}) collective-permute-start(f32[5,80,128]{2,1,0:T(8,128)S(1)} %get-tuple-element.56), channel_id=1, source_target_pairs={{0,1},{1,2},{2,3},{3,4},{4,5},{5,6},{6,7},{7,0},{8,9},{9,10},{10,1... | collective-permute-start | bytes 614408 | tf_op jit(solution)/shard_map/ppermute | solution.py:964
  25.5 5.5 %collective-permute-start.5 = (f32[5,80,128]{2,1,0:T(8,128)S(1)}, f32[5,80,128]{2,1,0:T(8,128)S(1)}, u32[]{:S(2)}, u32[]{:S(2)}) collective-permute-start(f32[5,80,128]{2,1,0:T(8,128)S(1)} %get-tuple-element.57), channel_id=1, source_target_pairs={{1,0},{2,1},{3,2},{4,3},{5,4},{6,5},{7,6},{0,7},{9,8},{10,9},{11,1... | collective-permute-start | bytes 614408 | tf_op jit(solution)/shard_map/ppermute | solution.py:963
  35.0 5.4 %collective-permute-start.6 = (f32[4,32,128]{2,1,0:T(8,128)S(1)}, f32[4,32,128]{2,1,0:T(8,128)S(1)}, u32[]{:S(2)}, u32[]{:S(2)}) collective-permute-start(f32[4,32,128]{2,1,0:T(8,128)S(1)} %get-tuple-element.62.high_quads), channel_id=1, source_target_pairs={{0,64},{64,128},{128,192},{192,256},{256,320},{320,384},{384,448},... | collective-permute-start | bytes 196616 | tf_op jit(solution)/shard_map/ppermute | solution.py:964
  39.1 5.4 %collective-permute-start.7 = (f32[4,32,128]{2,1,0:T(8,128)S(1)}, f32[4,32,128]{2,1,0:T(8,128)S(1)}, u32[]{:S(2)}, u32[]{:S(2)}) collective-permute-start(f32[4,32,128]{2,1,0:T(8,128)S(1)} %get-tuple-element.63.low_quads.after), channel_id=1, source_target_pairs={{64,0},{128,64},{192,128},{256,192},{320,256},{384,320},{448,384},... | collective-permute-start | bytes 196616 | tf_op jit(solution)/shard_map/ppermute | solution.py:963
  44.5 5.1 %collective-permute-start.8 = (f32[16,16,128]{2,1,0:T(8,128)S(1)}, f32[16,16,128]{2,1,0:T(8,128)S(1)}, u32[]{:S(2)}, u32[]{:S(2)}) collective-permute-start(f32[16,16,128]{2,1,0:T(8,128)S(1)} %pad_maximum_fusion), channel_id=1, source_target_pairs={{0,8},{8,16},{16,24},{24,32},{32,40},{40,48},{48,56},{1,9},{9,17},... | collective-permute-start | bytes 393224 | tf_op jit(solution)/shard_map/ppermute | solution.py:964
  47.7 6.7 %collective-permute-start.9 = (f32[16,16,128]{2,1,0:T(8,128)S(1)}, f32[16,16,128]{2,1,0:T(8,128)S(1)}, u32[]{:S(2)}, u32[]{:S(2)}) collective-permute-start(f32[16,16,128]{2,1,0:T(8,128)S(1)} %pad_maximum_fusion.1), channel_id=1, source_target_pairs={{8,0},{16,8},{24,16},{32,24},{40,32},{48,40},{56,48},{9,1},{17,9},... | collective-permute-start | bytes 393224 | tf_op jit(solution)/shard_map/ppermute | solution.py:963
  54.8 6.2 %collective-permute-start.10 = (f32[8,64,128]{2,1,0:T(8,128)S(1)}, f32[8,64,128]{2,1,0:T(8,128)S(1)}, u32[]{:S(2)}, u32[]{:S(2)}) collective-permute-start(f32[8,64,128]{2,1,0:T(8,128)S(1)} %get-tuple-element.64), channel_id=1, source_target_pairs={{0,1},{1,2},{2,3},{3,4},{4,5},{5,6},{6,7},{7,0},{8,9},{9,10},{10,1... | collective-permute-start | bytes 786440 | tf_op jit(solution)/shard_map/ppermute | solution.py:964
  57.7 5.9 %collective-permute-start.11 = (f32[8,64,128]{2,1,0:T(8,128)S(1)}, f32[8,64,128]{2,1,0:T(8,128)S(1)}, u32[]{:S(2)}, u32[]{:S(2)}) collective-permute-start(f32[8,64,128]{2,1,0:T(8,128)S(1)} %get-tuple-element.65), channel_id=1, source_target_pairs={{1,0},{2,1},{3,2},{4,3},{5,4},{6,5},{7,6},{0,7},{9,8},{10,9},{11,1... | collective-permute-start | bytes 786440 | tf_op jit(solution)/shard_map/ppermute | solution.py:963

commit v2 on v1

--- a/solution.py
+++ b/solution.py
@@ -514,7 +514,7 @@
 
 def fine_kernel(
     black0, g_red0, g_black0, kb, ka, c_ref, d_ref, weights, lanes, v_black, g_red, g_black, low_quads, high_quads,
-    black, red, rest, z_ref, planes, natural, later,
+    black, red, rest, z_ref, planes, natural, later, held,
 ):
     edges = block_edges()
     zero = jnp.zeros((80, 128), F32)
@@ -527,7 +527,7 @@
         return below, jnp.where(edges.khi, 0.0, gather_rows(ka, u, 80))
 
     def merge(p):
-        below, above = sides(p // 8)
+        below, above = held[2 * (p // 8)], held[2 * (p // 8) + 1]
         turned = 8 * (p % 8)
         place = (lane - turned) & 127
         edge = jnp.where(place < 5, above, jnp.where((place >= 59) & (place < 64), below, 0.0))
@@ -536,8 +536,7 @@
         g_red[p + 1] = g_red0[p + 1] + turn(edge, -turned, 1)
 
     def merge_black(n):
-        above = jnp.where(edges.khi, 0.0, gather_rows(ka, n // 8, 80))
-        below = later[n // 8]
+        below, above = later[n // 8], held[2 * (n // 8) + 1]
         turned = 8 * (n % 8)
         place = (lane - turned) & 127
         edge = jnp.where((place >= 5) & (place < 8), above, jnp.where((place >= 66) & (place < 69), below, 0.0))
@@ -545,8 +544,10 @@
         edge = jnp.where((place >= 69) & (place < 72), above, jnp.where((place >= 2) & (place < 5), below, 0.0))
         g_black[2 * n + 3] = g_black0[2 * n + 3] + turn(edge, -5 - turned, 1)
 
-    for u in range(3):
-        later[u] = turn(sides(u)[0], 2, 1)
+    for u in range(5):
+        held[2 * u], held[2 * u + 1] = sides(u)
+        if u < 3:
+            later[u] = turn(held[2 * u], 2, 1)
     for q in (0, 1, 38, 39, 40, 41):
         g_black[q] = zero
     for ref in (black, g_red):
@@ -915,7 +916,7 @@
                 send(out_held, out, p // 4 - 1)
         p = n - 6
         if 3 <= p < 35:
-            store(rest_held, p, red_rest(L0, edges, d0, gr0, red0, b0, p, even0), y0[p + 1])
+            store(rest_held, p, red_rest(L0, edges, d0, gr0, red0, b0, p, even0, lanes), y0[p + 1])
             if p % 4 == 2:
                 send(rest_held, rest, p // 4 - 1)
 
@@ -1003,7 +1004,7 @@
     v0, gr0, gb0, low_quads, high_quads = call(
         fine_kernel,
         (field, field, field, struct(4, 32, 128), struct(4, 32, 128)),
-        [fine, fine, fine, (32, 40, 128), (32, 40, 128), (8, 40, 128), (3, 80, 128)],
+        [fine, fine, fine, (32, 40, 128), (32, 40, 128), (8, 40, 128), (3, 80, 128), (10, 80, 128)],
     )(black, g_red, g_black, kb, ka, c0, d0, w0, lanes)
 
     ib, ia = pair(high_quads, low_quads, "gx")

time: 118 us -> 118 us (level)
  no operation moved by 1% of the time
where the time goes in v2:
time: 118 us
  blocking collectives  41.5 us (35%)
  starting transfers between devices  29.9 us (25%)
  Pallas kernels  21.7 us (18%)
  waiting for transfers between devices  21 us (18%)
  other arithmetic  1.65 us (1%)
    ppermute x6, starting transfers between devices, pair(): before = lax.ppermute(to_next, axis, up)  23.1 us
    pallas_call x11, Pallas kernels, run(): pl.pallas_call(kernel, out_shape=outs, in_specs=[space] * len(args), out_...  21.7 us
    all_to_all x1, blocking collectives, per_device(): tiles = lax.all_to_all(message, ('gy', 'gz'), 0, 0)  21.4 us
    all_to_all x1, blocking collectives, per_device(): tiles = lax.all_to_all(message, 'gx', 0, 0)  20.1 us
    ppermute x6, waiting for transfers between devices, pair(): after = lax.ppermute(to_before, axis, down)  17.1 us
    ppermute x6, starting transfers between devices, pair(): after = lax.ppermute(to_before, axis, down)  6.79 us
    ppermute x6, waiting for transfers between devices, pair(): before = lax.ppermute(to_next, axis, up)  3.92 us
  transfers between devices with their start and end apart: 12, of which 8 were waited for; matrix products, arithmetic and copies ran while one was open for 1% of the time, Pallas kernels for 3%

profile of v2, /device:TPU:1, one launch (start us, length us, event | category | flops | bytes accessed | tf_op | source)
XLA Modules:
  0.0 118.0 jit_solution(4620954229814970165)
XLA Ops:
  0.7 1.4 %slice_select_fusion = (f32[3,64,64]{2,1,0:T(8,128)S(1)}, f32[3,64,64]{2,1,0:T(8,128)S(1)}, f32[3,64,64]{2,1,0:T(8,128)S(1)}, f32[3,64,64]{2,1,0:T(8,128)S(1)}, ...) fusion(f32[64,64,64]{2,1,0:T(8,128)} %guess.1, pred[64,64]{1,0:T(8,128)(4,1)S(1)} %and_compare_fusion, ...), kind=kLoop, calls=%fused_computation.4 | loop fusion | flops 73728 | bytes 692224 | tf_op jit(solution)/shard_map/jit(_where)/select_n | solution.py:975
  2.2 1.4 %collective-permute-start.1 = (f32[4,64,128]{2,1,0:T(8,128)S(1)}, f32[4,64,128]{2,1,0:T(8,128)S(1)}, u32[]{:S(2)}, u32[]{:S(2)}) collective-permute-start(f32[4,64,128]{2,1,0:T(8,128)S(1)} %maximum_maximum_fusion.1), channel_id=1, source_target_pairs={{64,0},{128,64},{192,128},{256,192},{320,256},{384,320},{448,384},... | collective-permute-start | bytes 393224 | tf_op jit(solution)/shard_map/ppermute | solution.py:964
  3.8 5.5 %collective-permute-start = (f32[4,64,128]{2,1,0:T(8,128)S(1)}, f32[4,64,128]{2,1,0:T(8,128)S(1)}, u32[]{:S(2)}, u32[]{:S(2)}) collective-permute-start(f32[4,64,128]{2,1,0:T(8,128)S(1)} %maximum_maximum_fusion), channel_id=1, source_target_pairs={{0,64},{64,128},{128,192},{192,256},{256,320},{320,384},{384,448},... | collective-permute-start | bytes 393224 | tf_op jit(solution)/shard_map/ppermute | solution.py:965
  9.2 1.1 fusion
  10.4 0.8 collective-permute-done.ib
  11.3 3.4 %collective-permute-start.2 = (f32[248,128]{1,0:T(8,128)S(1)}, f32[248,128]{1,0:T(8,128)S(1)}, u32[]{:S(2)}, u32[]{:S(2)}) collective-permute-start(f32[248,128]{1,0:T(8,128)S(1)} %get-tuple-element.49), channel_id=1, source_target_pairs={{0,8},{8,16},{16,24},{24,32},{32,40},{40,48},{48,56},{1,9},{9,17},... | collective-permute-start | bytes 380936 | tf_op jit(solution)/shard_map/ppermute | solution.py:965
  14.8 1.3 %collective-permute-start.3 = (f32[248,128]{1,0:T(8,128)S(1)}, f32[248,128]{1,0:T(8,128)S(1)}, u32[]{:S(2)}, u32[]{:S(2)}) collective-permute-start(f32[248,128]{1,0:T(8,128)S(1)} %get-tuple-element.50), channel_id=1, source_target_pairs={{8,0},{16,8},{24,16},{32,24},{40,32},{48,40},{56,48},{9,1},{17,9},... | collective-permute-start | bytes 380936 | tf_op jit(solution)/shard_map/ppermute | solution.py:964
  16.1 1.0 shard_map.41
  17.1 3.4 %collective-permute-done.3.ja = f32[248,128]{1,0:T(8,128)S(1)} collective-permute-done((f32[248,128]{1,0:T(8,128)S(1)}, f32[248,128]{1,0:T(8,128)S(1)}, u32[]{:S(2)}, u32[]{:S(2)}) %collective-permute-start.3) | collective-permute-done | bytes 127008 | tf_op jit(solution)/shard_map/ppermute | solution.py:964
  20.4 1.0 shard_map.43
  21.4 4.1 %collective-permute-start.4 = (f32[5,80,128]{2,1,0:T(8,128)S(1)}, f32[5,80,128]{2,1,0:T(8,128)S(1)}, u32[]{:S(2)}, u32[]{:S(2)}) collective-permute-start(f32[5,80,128]{2,1,0:T(8,128)S(1)} %get-tuple-element.56), channel_id=1, source_target_pairs={{0,1},{1,2},{2,3},{3,4},{4,5},{5,6},{6,7},{7,0},{8,9},{9,10},{10,1... | collective-permute-start | bytes 614408 | tf_op jit(solution)/shard_map/ppermute | solution.py:965
  25.5 1.5 %collective-permute-start.5 = (f32[5,80,128]{2,1,0:T(8,128)S(1)}, f32[5,80,128]{2,1,0:T(8,128)S(1)}, u32[]{:S(2)}, u32[]{:S(2)}) collective-permute-start(f32[5,80,128]{2,1,0:T(8,128)S(1)} %get-tuple-element.57), channel_id=1, source_target_pairs={{1,0},{2,1},{3,2},{4,3},{5,4},{6,5},{7,6},{0,7},{9,8},{10,9},{11,1... | collective-permute-start | bytes 614408 | tf_op jit(solution)/shard_map/ppermute | solution.py:964
  27.0 1.7 %shard_map.44 = (f32[42,80,128]{2,1,0:T(8,128)S(1)}, f32[42,80,128]{2,1,0:T(8,128)S(1)}, f32[42,80,128]{2,1,0:T(8,128)S(1)}, f32[4,80,128]{2,1,0:T(8,128)S(1)}, ...) custom-call(f32[40,80,128]{2,1,0:T(8,128)S(1)} %get-tuple-element.51.xf, ...), custom_call_target="tpu_custom_call" | custom-call | flops 2000000 | bytes 1000000 | tf_op jit(solution)/shard_map/pallas_call | solution.py:948
  28.7 2.3 %collective-permute-done.5.ka = f32[5,80,128]{2,1,0:T(8,128)S(1)} collective-permute-done((f32[5,80,128]{2,1,0:T(8,128)S(1)}, f32[5,80,128]{2,1,0:T(8,128)S(1)}, u32[]{:S(2)}, u32[]{:S(2)}) %collective-permute-start.5) | collective-permute-done | bytes 204832 | tf_op jit(solution)/shard_map/ppermute | solution.py:964
  31.0 3.9 %shard_map.45 = (f32[42,80,128]{2,1,0:T(8,128)S(1)}, f32[42,80,128]{2,1,0:T(8,128)S(1)}, f32[42,80,128]{2,1,0:T(8,128)S(1)}, f32[4,32,128]{2,1,0:T(8,128)S(1)}, f32[4,32,128]{2,1,0:T(8,128)S(1)}) custom-call(f32[42,80,128]{2,1,0:T(8,128)S(1)} %get-tuple-element.53.black0, f32[42,80,128]{2,1,0:T(8,128)S(1)} %get-tuple-element.54.g_red0, ...), custom_call_target="tpu_custom_call" | custom-call | flops 2000000 | bytes 1000000 | tf_op jit(solution)/shard_map/pallas_call | solution.py:948
  34.9 4.1 %collective-permute-start.6 = (f32[4,32,128]{2,1,0:T(8,128)S(1)}, f32[4,32,128]{2,1,0:T(8,128)S(1)}, u32[]{:S(2)}, u32[]{:S(2)}) collective-permute-start(f32[4,32,128]{2,1,0:T(8,128)S(1)} %get-tuple-element.62.high_quads), channel_id=1, source_target_pairs={{0,64},{64,128},{128,192},{192,256},{256,320},{320,384},{384,448},... | collective-permute-start | bytes 196616 | tf_op jit(solution)/shard_map/ppermute | solution.py:965
  39.0 1.3 %collective-permute-start.7 = (f32[4,32,128]{2,1,0:T(8,128)S(1)}, f32[4,32,128]{2,1,0:T(8,128)S(1)}, u32[]{:S(2)}, u32[]{:S(2)}) collective-permute-start(f32[4,32,128]{2,1,0:T(8,128)S(1)} %get-tuple-element.63.low_quads.after), channel_id=1, source_target_pairs={{64,0},{128,64},{192,128},{256,192},{320,256},{384,320},{448,384},... | collective-permute-start | bytes 196616 | tf_op jit(solution)/shard_map/ppermute | solution.py:964
  40.4 4.0 %collective-permute-done.7.ia = f32[4,32,128]{2,1,0:T(8,128)S(1)} collective-permute-done((f32[4,32,128]{2,1,0:T(8,128)S(1)}, f32[4,32,128]{2,1,0:T(8,128)S(1)}, u32[]{:S(2)}, u32[]{:S(2)}) %collective-permute-start.7) | collective-permute-done | bytes 65568 | tf_op jit(solution)/shard_map/ppermute | solution.py:964
  44.4 3.2 %collective-permute-start.8 = (f32[16,16,128]{2,1,0:T(8,128)S(1)}, f32[16,16,128]{2,1,0:T(8,128)S(1)}, u32[]{:S(2)}, u32[]{:S(2)}) collective-permute-start(f32[16,16,128]{2,1,0:T(8,128)S(1)} %pad_maximum_fusion), channel_id=1, source_target_pairs={{0,8},{8,16},{16,24},{24,32},{32,40},{40,48},{48,56},{1,9},{9,17},... | collective-permute-start | bytes 393224 | tf_op jit(solution)/shard_map/ppermute | solution.py:965
  47.6 1.3 %collective-permute-start.9 = (f32[16,16,128]{2,1,0:T(8,128)S(1)}, f32[16,16,128]{2,1,0:T(8,128)S(1)}, u32[]{:S(2)}, u32[]{:S(2)}) collective-permute-start(f32[16,16,128]{2,1,0:T(8,128)S(1)} %pad_maximum_fusion.1), channel_id=1, source_target_pairs={{8,0},{16,8},{24,16},{32,24},{40,32},{48,40},{56,48},{9,1},{17,9},... | collective-permute-start | bytes 393224 | tf_op jit(solution)/shard_map/ppermute | solution.py:964
  48.9 0.6 collective-permute-done.8.jb
  49.6 4.8 %collective-permute-done.9.ja = f32[16,16,128]{2,1,0:T(8,128)S(1)} collective-permute-done((f32[16,16,128]{2,1,0:T(8,128)S(1)}, f32[16,16,128]{2,1,0:T(8,128)S(1)}, u32[]{:S(2)}, u32[]{:S(2)}) %collective-permute-start.9) | collective-permute-done | bytes 131104 | tf_op jit(solution)/shard_map/ppermute | solution.py:964
  54.4 0.3 shard_map.47
  54.7 2.9 %collective-permute-start.10 = (f32[8,64,128]{2,1,0:T(8,128)S(1)}, f32[8,64,128]{2,1,0:T(8,128)S(1)}, u32[]{:S(2)}, u32[]{:S(2)}) collective-permute-start(f32[8,64,128]{2,1,0:T(8,128)S(1)} %get-tuple-element.64), channel_id=1, source_target_pairs={{0,1},{1,2},{2,3},{3,4},{4,5},{5,6},{6,7},{7,0},{8,9},{9,10},{10,1... | collective-permute-start | bytes 786440 | tf_op jit(solution)/shard_map/ppermute | solution.py:965
  57.6 0.8 shard_map.48
  58.4 2.5 %collective-permute-done.10.kb = f32[8,64,128]{2,1,0:T(8,128)S(1)} collective-permute-done((f32[8,64,128]{2,1,0:T(8,128)S(1)}, f32[8,64,128]{2,1,0:T(8,128)S(1)}, u32[]{:S(2)}, u32[]{:S(2)}) %collective-permute-start.10) | collective-permute-done | bytes 262176 | tf_op jit(solution)/shard_map/ppermute | solution.py:965
  60.9 2.6 %collective-permute-done.11.ka = f32[8,64,128]{2,1,0:T(8,128)S(1)} collective-permute-done((f32[8,64,128]{2,1,0:T(8,128)S(1)}, f32[8,64,128]{2,1,0:T(8,128)S(1)}, u32[]{:S(2)}, u32[]{:S(2)}) %collective-permute-start.11) | collective-permute-done | bytes 262176 | tf_op jit(solution)/shard_map/ppermute | solution.py:964
  63.5 3.0 %shard_map.49 = (f32[32,64,128]{2,1,0:T(8,128)S(1)}, f32[32,64,128]{2,1,0:T(8,128)S(1)}, f32[32,64,128]{2,1,0:T(8,128)S(1)}, f32[16,32,128]{2,1,0:T(8,128)S(1)},...) custom-call(f32[16,64,128]{2,1,0:T(8,128)S(1)} %shard_map.46.qf, ...), custom_call_target="tpu_custom_call" | custom-call | flops 2000000 | bytes 1000000 | tf_op jit(solution)/shard_map/pallas_call | solution.py:948
  66.5 21.4 %all_to_all.10.tiles = f32[64,5,1,128]{3,2,1,0:T(1,128)S(1)} all-to-all(f32[64,5,1,128]{3,2,1,0:T(1,128)S(1)} %get-tuple-element.73), channel_id=1, replica_groups=mesh['gx'=8,'gy'=8,'gz'=8] {'gy','gz'}, dimensions={0} | all-to-all | bytes 327680 | tf_op jit(solution)/shard_map/all_to_all | solution.py:1032
  87.9 0.4 shard_map.50
  88.3 20.1 %all_to_all.11.tiles = f32[8,56,128]{2,1,0:T(8,128)S(1)} all-to-all(f32[8,56,128]{2,1,0:T(8,128)S(1)} %get-tuple-element.74), channel_id=1, replica_groups=mesh['gx'=8,'gy'=8,'gz'=8] {'gx'}, dimensions={0} | all-to-all | bytes 458752 | tf_op jit(solution)/shard_map/all_to_all | solution.py:1036
  108.4 9.5 %shard_map.51 = (f32[64,64,64]{2,1,0:T(8,128)}, f32[64,64,64]{2,1,0:T(8,128)}) custom-call(f32[8,56,128]{2,1,0:T(8,128)S(1)} %all_to_all.11.tiles, f32[8,24,128]{2,1,0:T(8,128)S(1)} %get-tuple-element.75.near, f32[16,32,128]{2,1,0:T(8,128)S(1)} %get-tuple-element.76.v2, f32[16,32,128]{2,1,0:T(8,128)S(1)} %get-tuple-element.77.gr2, ...), custom_call_target="tpu_custom_call" | custom-call | flops 2000000 | bytes 1000000 | tf_op jit(solution)/shard_map/pallas_call | solution.py:948
  (22 shorter events, 0.5 us)
Async XLA Ops:
  0.6 8.6 %copy-start = (f32[64,64,64]{2,1,0:T(8,128)S(1)}, f32[64,64,64]{2,1,0:T(8,128)}, u32[]{:S(2)}) copy-start(f32[64,64,64]{2,1,0:T(8,128)} %guess.1) | copy-start | bytes 3145732
  2.1 14.0 %copy-start.1 = (f32[64,64,64]{2,1,0:T(8,128)S(1)}, f32[64,64,64]{2,1,0:T(8,128)}, u32[]{:S(2)}) copy-start(f32[64,64,64]{2,1,0:T(8,128)} %source.1) | copy-start | bytes 3145732
  2.2 8.1 %collective-permute-start.1 = (f32[4,64,128]{2,1,0:T(8,128)S(1)}, f32[4,64,128]{2,1,0:T(8,128)S(1)}, u32[]{:S(2)}, u32[]{:S(2)}) collective-permute-start(f32[4,64,128]{2,1,0:T(8,128)S(1)} %maximum_maximum_fusion.1), channel_id=1, source_target_pairs={{64,0},{128,64},{192,128},{256,192},{320,256},{384,320},{448,384},... | collective-permute-start | bytes 393224 | tf_op jit(solution)/shard_map/ppermute | solution.py:964
  3.8 7.4 %collective-permute-start = (f32[4,64,128]{2,1,0:T(8,128)S(1)}, f32[4,64,128]{2,1,0:T(8,128)S(1)}, u32[]{:S(2)}, u32[]{:S(2)}) collective-permute-start(f32[4,64,128]{2,1,0:T(8,128)S(1)} %maximum_maximum_fusion), channel_id=1, source_target_pairs={{0,64},{64,128},{128,192},{192,256},{256,320},{320,384},{384,448},... | collective-permute-start | bytes 393224 | tf_op jit(solution)/shard_map/ppermute | solution.py:965
  11.3 5.7 %collective-permute-start.2 = (f32[248,128]{1,0:T(8,128)S(1)}, f32[248,128]{1,0:T(8,128)S(1)}, u32[]{:S(2)}, u32[]{:S(2)}) collective-permute-start(f32[248,128]{1,0:T(8,128)S(1)} %get-tuple-element.49), channel_id=1, source_target_pairs={{0,8},{8,16},{16,24},{24,32},{32,40},{40,48},{48,56},{1,9},{9,17},... | collective-permute-start | bytes 380936 | tf_op jit(solution)/shard_map/ppermute | solution.py:965
  14.8 5.7 %collective-permute-start.3 = (f32[248,128]{1,0:T(8,128)S(1)}, f32[248,128]{1,0:T(8,128)S(1)}, u32[]{:S(2)}, u32[]{:S(2)}) collective-permute-start(f32[248,128]{1,0:T(8,128)S(1)} %get-tuple-element.50), channel_id=1, source_target_pairs={{8,0},{16,8},{24,16},{32,24},{40,32},{48,40},{56,48},{9,1},{17,9},... | collective-permute-start | bytes 380936 | tf_op jit(solution)/shard_map/ppermute | solution.py:964
  21.4 7.3 %collective-permute-start.4 = (f32[5,80,128]{2,1,0:T(8,128)S(1)}, f32[5,80,128]{2,1,0:T(8,128)S(1)}, u32[]{:S(2)}, u32[]{:S(2)}) collective-permute-start(f32[5,80,128]{2,1,0:T(8,128)S(1)} %get-tuple-element.56), channel_id=1, source_target_pairs={{0,1},{1,2},{2,3},{3,4},{4,5},{5,6},{6,7},{7,0},{8,9},{9,10},{10,1... | collective-permute-start | bytes 614408 | tf_op jit(solution)/shard_map/ppermute | solution.py:965
  25.5 5.5 %collective-permute-start.5 = (f32[5,80,128]{2,1,0:T(8,128)S(1)}, f32[5,80,128]{2,1,0:T(8,128)S(1)}, u32[]{:S(2)}, u32[]{:S(2)}) collective-permute-start(f32[5,80,128]{2,1,0:T(8,128)S(1)} %get-tuple-element.57), channel_id=1, source_target_pairs={{1,0},{2,1},{3,2},{4,3},{5,4},{6,5},{7,6},{0,7},{9,8},{10,9},{11,1... | collective-permute-start | bytes 614408 | tf_op jit(solution)/shard_map/ppermute | solution.py:964
  34.9 5.4 %collective-permute-start.6 = (f32[4,32,128]{2,1,0:T(8,128)S(1)}, f32[4,32,128]{2,1,0:T(8,128)S(1)}, u32[]{:S(2)}, u32[]{:S(2)}) collective-permute-start(f32[4,32,128]{2,1,0:T(8,128)S(1)} %get-tuple-element.62.high_quads), channel_id=1, source_target_pairs={{0,64},{64,128},{128,192},{192,256},{256,320},{320,384},{384,448},... | collective-permute-start | bytes 196616 | tf_op jit(solution)/shard_map/ppermute | solution.py:965
  39.0 5.4 %collective-permute-start.7 = (f32[4,32,128]{2,1,0:T(8,128)S(1)}, f32[4,32,128]{2,1,0:T(8,128)S(1)}, u32[]{:S(2)}, u32[]{:S(2)}) collective-permute-start(f32[4,32,128]{2,1,0:T(8,128)S(1)} %get-tuple-element.63.low_quads.after), channel_id=1, source_target_pairs={{64,0},{128,64},{192,128},{256,192},{320,256},{384,320},{448,384},... | collective-permute-start | bytes 196616 | tf_op jit(solution)/shard_map/ppermute | solution.py:964
  44.4 5.1 %collective-permute-start.8 = (f32[16,16,128]{2,1,0:T(8,128)S(1)}, f32[16,16,128]{2,1,0:T(8,128)S(1)}, u32[]{:S(2)}, u32[]{:S(2)}) collective-permute-start(f32[16,16,128]{2,1,0:T(8,128)S(1)} %pad_maximum_fusion), channel_id=1, source_target_pairs={{0,8},{8,16},{16,24},{24,32},{32,40},{40,48},{48,56},{1,9},{9,17},... | collective-permute-start | bytes 393224 | tf_op jit(solution)/shard_map/ppermute | solution.py:965
  47.6 6.7 %collective-permute-start.9 = (f32[16,16,128]{2,1,0:T(8,128)S(1)}, f32[16,16,128]{2,1,0:T(8,128)S(1)}, u32[]{:S(2)}, u32[]{:S(2)}) collective-permute-start(f32[16,16,128]{2,1,0:T(8,128)S(1)} %pad_maximum_fusion.1), channel_id=1, source_target_pairs={{8,0},{16,8},{24,16},{32,24},{40,32},{48,40},{56,48},{9,1},{17,9},... | collective-permute-start | bytes 393224 | tf_op jit(solution)/shard_map/ppermute | solution.py:964
  54.7 6.2 %collective-permute-start.10 = (f32[8,64,128]{2,1,0:T(8,128)S(1)}, f32[8,64,128]{2,1,0:T(8,128)S(1)}, u32[]{:S(2)}, u32[]{:S(2)}) collective-permute-start(f32[8,64,128]{2,1,0:T(8,128)S(1)} %get-tuple-element.64), channel_id=1, source_target_pairs={{0,1},{1,2},{2,3},{3,4},{4,5},{5,6},{6,7},{7,0},{8,9},{9,10},{10,1... | collective-permute-start | bytes 786440 | tf_op jit(solution)/shard_map/ppermute | solution.py:965
  57.6 5.9 %collective-permute-start.11 = (f32[8,64,128]{2,1,0:T(8,128)S(1)}, f32[8,64,128]{2,1,0:T(8,128)S(1)}, u32[]{:S(2)}, u32[]{:S(2)}) collective-permute-start(f32[8,64,128]{2,1,0:T(8,128)S(1)} %get-tuple-element.65), channel_id=1, source_target_pairs={{1,0},{2,1},{3,2},{4,3},{5,4},{6,5},{7,6},{0,7},{9,8},{10,9},{11,1... | collective-permute-start | bytes 786440 | tf_op jit(solution)/shard_map/ppermute | solution.py:964
